TPU v7x, 32 devices: a whole 2x2x4 slice. The times are simulated.
32 devices in a mesh: tp: 4 (over z), side: 2 (over y), rep: 4 (over x, core).
Axes of the slice: x: 2, y: 2, z: 4, core: 2. Of those that a mesh axis runs over, the one named last changes fastest.
Arguments:
- w_up: float32 [2, 1, 2048, 8192], P('side', None, ('rep', 'tp'))
- w_down: float32 [2, 1, 8192, 2048], P('side', None, None, ('rep', 'tp'))
- g_up: float32 [2, 1, 2048, 8192], P('side', None, ('rep', 'tp'))
- g_down: float32 [2, 1, 8192, 2048], P('side', None, None, ('rep', 'tp'))
- learn_rate: float32 [2], P('side')
- prompts: bfloat16 [2, 4, 8192, 2048], P('side', 'rep')
Outputs:
- output 1: float32 [2, 1, 2048, 8192], P('side', None, ('rep', 'tp'))
- output 2: float32 [2, 1, 8192, 2048], P('side', None, None, ('rep', 'tp'))
- output 3: bfloat16 [2, 4, 8192, 2048], P('side', 'rep')
All inputs are finite; a program needn't handle non-finite values.
Results may differ from a plain program's by a relative error of at most 0.001.
Values are sent between devices in bfloat16 or wider.
A program may use at most 1 GiB of HBM per device.

v0:
```python
import jax
import jax.numpy as jnp
from jax import lax
from jax.sharding import PartitionSpec as P


def solution(mesh):
    up_spec = P("side", None, ("rep", "tp"), None)
    down_spec = P("side", None, None, ("rep", "tp"))
    tok_spec = P("side", "rep", None, None)

    def device_step(w_up, w_down, g_up, g_down, learn_rate, prompts):
        is_trainer = lax.axis_index("side") == 0
        rate = learn_rate[0]
        new_up = jnp.where(is_trainer, w_up - rate * g_up, 0.0)
        new_down = jnp.where(is_trainer, w_down - rate * g_down, 0.0)
        recv_up = lax.ppermute(new_up[0].astype(jnp.bfloat16), "side", perm=[(0, 1)])
        recv_down = lax.ppermute(new_down[0].astype(jnp.bfloat16), "side", perm=[(0, 1)])
        band_up = lax.all_to_all(recv_up, "tp", 2, 1, tiled=True)
        band_down = lax.all_to_all(recv_down, "tp", 1, 2, tiled=True)
        full_up = lax.all_gather(band_up, "rep", axis=1, tiled=True)
        full_down = lax.all_gather(band_down, "rep", axis=2, tiled=True)
        hidden = prompts[0, 0]
        for layer in range(full_up.shape[0]):
            pre_act = jnp.dot(hidden, full_up[layer], preferred_element_type=jnp.float32)
            act_up = jax.nn.gelu(pre_act, approximate=True).astype(jnp.bfloat16)
            part_sum = jnp.dot(act_up, full_down[layer], preferred_element_type=jnp.float32)
            part_sum = lax.psum(part_sum, "tp")
            hidden = (hidden.astype(jnp.float32) + part_sum).astype(jnp.bfloat16)
        gen_out = jnp.where(is_trainer, jnp.zeros_like(hidden), hidden)
        return new_up, new_down, gen_out[None, None]

    return jax.shard_map(
        device_step,
        mesh=mesh,
        in_specs=(up_spec, down_spec, up_spec, down_spec, P("side"), tok_spec),
        out_specs=(up_spec, down_spec, tok_spec),
        check_vma=False,
    )
```

profile of v0, /device:TPU:4, one launch (start us, length us, event | category | flops | bytes accessed | tf_op | source)
XLA Modules:
  0.0 2779.6 jit_solution(688395451990489296)
XLA Ops:
  7.2 0.0 all-gather.3.cloned.1.call-start
  7.9 6.2 convert_bitcast_fusion.1
  14.1 1.3 collective-permute-start
  15.4 48.0 %collective-permute-done = bf16[1,128,8192]{2,1,0:T(8,128)(2,1)S(1)} collective-permute-done((bf16[1,128,8192]{2,1,0:T(8,128)(2,1)S(1)}, bf16[1,128,8192]{2,1,0:T(8,128)(2,1)S(1)}, u32[]{:S(2)}, u32[]{:S(2)}) %collective-permute-start) | collective-permute-done | bytes 2097184 | tf_op jit(solution)/shard_map/ppermute | solution.py:17
  63.3 6.8 copy.19
  70.1 0.5 broadcast
  70.6 45.1 %reduce.1 = bf16[8192,128]{1,0:T(8,128)(2,1)S(1)} reduce(bf16[8192,1,128]{2,1,0:T(2,128)(2,1)} %bitcast.51, bf16[]{:T(256)} %broadcast), dimensions={1}, to_apply=%bitcast.34.reduce_sub_computation | reduce | bytes 4194306
  115.7 2.1 reshape.34
  117.8 52.5 %all_to_all.36 = bf16[4,2,131072]{2,1,0:T(2,128)(2,1)S(1)} all-to-all(bf16[4,2,131072]{2,1,0:T(2,128)(2,1)} %reshape.34), channel_id=1, replica_groups=mesh['tp'=4,'side'=2,'rep'=4] {'tp'}, dimensions={0} | all-to-all | bytes 4194304 | tf_op jit(solution)/shard_map/all_to_all | solution.py:19
  170.3 3.3 reshape.35
  173.6 2.5 copy.23
  176.1 2.7 copy.20
  178.8 0.0 all-gather.3.cloned.1.call-update
  178.8 0.0 all-gather.5.cloned.1.call-start
  178.9 6.1 convert_bitcast_fusion
  184.9 1.5 collective-permute-start.1
  186.4 47.4 %collective-permute-done.1 = bf16[1,8192,128]{2,1,0:T(8,128)(2,1)S(1)} collective-permute-done((bf16[1,8192,128]{2,1,0:T(8,128)(2,1)S(1)}, bf16[1,8192,128]{2,1,0:T(8,128)(2,1)S(1)}, u32[]{:S(2)}, u32[]{:S(2)}) %collective-permute-start.1) | collective-permute-done | bytes 2097184 | tf_op jit(solution)/shard_map/ppermute | solution.py:18
  233.8 33.2 %copy.26 = bf16[1,8192,128]{2,0,1:T(2,128)(2,1)} copy(bf16[1,8192,128]{2,1,0:T(8,128)(2,1)S(1)} %collective-permute-done.1) | data formatting | bytes 4194304 | tf_op jit(solution)/shard_map/ppermute | solution.py:18
  267.0 45.1 %reduce = bf16[8192,128]{1,0:T(8,128)(2,1)S(1)} reduce(bf16[8192,1,128]{2,1,0:T(2,128)(2,1)} %bitcast.52, bf16[]{:T(256)} %broadcast), dimensions={1}, to_apply=%bitcast.48.reduce_sub_computation | reduce | bytes 4194306
  312.1 2.1 reshape.32
  314.1 51.4 %all_to_all.37 = bf16[4,2,131072]{2,1,0:T(2,128)(2,1)S(1)} all-to-all(bf16[4,2,131072]{2,1,0:T(2,128)(2,1)} %reshape.32), channel_id=1, replica_groups=mesh['tp'=4,'side'=2,'rep'=4] {'tp'}, dimensions={0} | all-to-all | bytes 4194304 | tf_op jit(solution)/shard_map/all_to_all | solution.py:20
  365.5 3.3 reshape.33
  368.8 2.5 copy.24
  371.3 2.7 copy.22
  373.9 0.0 all-gather.5.cloned.1.call-update
  374.0 0.3 all-reduce.2.cloned.1.call-start
  374.2 0.0 all-gather.3.cloned.1.call-done
  374.3 96.6 %fusion.7.clone.4 = bf16[8192,2048]{0,1:T(8,128)(2,1)} fusion(bf16[1,1,8192,2048]{3,2,1,0:T(8,128)(2,1)} %param.11, bf16[1,2048,2048]{2,1,0:T(8,128)(2,1)} %all-gather.3.cloned.1.call-done), kind=kOutput, calls=%fused_computation.8.clone.clone.clone.1 | convolution fusion | flops 68870471680 | bytes 75497472 | tf_op jit(solution)/shard_map/dot_general | solution.py:25
  470.9 79.2 %fusion.12 = f32[8192,2048]{1,0:T(8,128)} fusion(bf16[1,2048,2048]{1,2,0:T(8,128)(2,1)} %all-gather.5.cloned.1.call-done, bf16[8192,2048]{0,1:T(8,128)(2,1)} %fusion.7.clone.4), kind=kOutput, calls=%fused_computation.13 | convolution fusion | flops 68719476736 | bytes 109051904 | tf_op jit(solution)/shard_map/dot_general | solution.py:27
  550.0 0.0 all-reduce.2.cloned.1.call-update
  550.1 2180.0 %all-reduce.2.cloned.1.call-done = f32[8192,2048]{1,0:T(8,128)} async-done(((f32[8192,2048]{1,0:T(8,128)}), f32[8192,2048]{1,0:T(8,128)}) %all-reduce.2.cloned.1.call-update) | async-done | bytes 67108880 | tf_op jit(solution)/shard_map/psum | solution.py:28
  2730.0 42.6 %fusion.9 = bf16[1,1,8192,2048]{3,2,1,0:T(8,128)(2,1)} fusion(f32[8192,2048]{1,0:T(8,128)} %all-reduce.2.cloned.1.call-done, bf16[1,1,8192,2048]{3,2,1,0:T(8,128)(2,1)} %param.11, pred[]{:T(512)S(6)} %eq.3), kind=kLoop, calls=%fused_computation.11 | loop fusion | flops 67108864 | bytes 134217728 | tf_op jit(solution)/shard_map/broadcast_in_dim | solution.py:31
  (1 shorter events, 0.0 us)
Async XLA Ops:
  7.2 367.1 %all-gather.3.cloned.1.call-start = ((), (), s32[]{:S(2)}) async-start(), calls=%async_computation.2 | async-start | bytes 10485760 | tf_op jit(solution)/shard_map/all_gather | solution.py:21
  14.1 49.3 %collective-permute-start = (bf16[1,128,8192]{2,1,0:T(8,128)(2,1)S(1)}, bf16[1,128,8192]{2,1,0:T(8,128)(2,1)S(1)}, u32[]{:S(2)}, u32[]{:S(2)}) collective-permute-start(bf16[1,128,8192]{2,1,0:T(8,128)(2,1)S(1)} %get-tuple-element.9), channel_id=1, source_target_pairs={{0,4},{1,5},{2,6},{3,7},{8,12},{9,13},{10,14},{11,15},{16,20},{17,... | collective-permute-start | bytes 6291464 | tf_op jit(solution)/shard_map/ppermute | solution.py:17
  178.8 292.1 %all-gather.5.cloned.1.call-start = ((), (), s32[]{:S(2)}) async-start(), calls=%async_computation.3 | async-start | bytes 10485760 | tf_op jit(solution)/shard_map/all_gather | solution.py:22
  184.9 48.8 %collective-permute-start.1 = (bf16[1,8192,128]{2,1,0:T(8,128)(2,1)S(1)}, bf16[1,8192,128]{2,1,0:T(8,128)(2,1)S(1)}, u32[]{:S(2)}, u32[]{:S(2)}) collective-permute-start(bf16[1,8192,128]{2,1,0:T(8,128)(2,1)S(1)} %get-tuple-element.11), channel_id=1, source_target_pairs={{0,4},{1,5},{2,6},{3,7},{8,12},{9,13},{10,14},{11,15},{16,20},{17,... | collective-permute-start | bytes 6291464 | tf_op jit(solution)/shard_map/ppermute | solution.py:18
  374.0 2356.1 %all-reduce.2.cloned.1.call-start = ((), (), s32[]{:S(2)}) async-start(), calls=%async_computation.4 | async-start | bytes 134217728 | tf_op jit(solution)/shard_map/psum | solution.py:28
Sparse Core Ops, SparseCore 0:
  178.9 57.1 all-gather.2
  374.1 56.9 all-gather.4
  550.2 2179.7 all-reduce.1
where the time goes:
time: 2790 us; the launch traced here: 2780 us
  waiting for transfers between devices  2280 us (82%)
  matrix products  176 us (6%)
  other arithmetic  145 us (5%)
  blocking collectives  104 us (4%)
  local copies, waits for them, and re-layouts  61.5 us (2%)
    psum x1, waiting for transfers between devices, device_step(): part_sum = lax.psum(part_sum, 'tp')  2180 us
    dot_general x1, matrix products, device_step(): jnp.dot(hidden, full_up[layer], preferred_element_type=jnp.float32)  96.6 us
    unnamed x2, other arithmetic  90.2 us
    dot_general x1, matrix products, device_step(): jnp.dot(act_up, full_down[layer], preferred_element_type=jnp.float32)  79.2 us
  transfers between devices with their start and end apart: 5, of which 3 were waited for; matrix products, arithmetic and copies ran while one was open for 7% of the time, Pallas kernels for 0%

commit v1 on v0

v1 whole, which is shorter than its diff:
```python
import functools
import math

import jax
import jax.numpy as jnp
from jax import lax
from jax.experimental import pallas as pl
from jax.experimental.pallas import tpu as pltpu
from jax.sharding import PartitionSpec as P

BF, F32 = jnp.bfloat16, jnp.float32
MESH = pl.DeviceIdType.MESH
D, F, TOK = 2048, 8192, 8192
FC = 256
NCH = F // FC
FS = 512
NST = F // FS
M = 1024
R1 = 3 * M
R2 = TOK - 2 * R1
PC = 256
NPC = R1 // PC
AHEAD = 3
LAGX, LAGD = 1, 3


def gelu(a):
    k = math.sqrt(2.0 / math.pi)
    half = 0.5 * a
    return half + half * jnp.tanh(a * (k + (k * 0.044715) * (a * a)))


def kernel(
    wu_in, wd_in, rows_in, out, w_all, relay, h, acc, wu, wd,
    y_sem, x_sem, b_sem, d_sem, s1, s2, s3, sb, ld_sem, h_sem, o_sem, e_recv, e_send, r_recv,
):
    t, side, r = lax.axis_index("tp"), lax.axis_index("side"), lax.axis_index("rep")
    x, c = r // 2, r % 2

    def send(src, dst, send_sem, recv_sem, device):
        pltpu.make_async_remote_copy(
            src, dst, send_sem, recv_sem, device_id=device, device_id_type=MESH
        ).start()

    def wait(ref, sem):
        pltpu.make_async_copy(ref, ref, sem).wait()

    def kind(ch):
        m = (ch * 7) % 16
        return m < 7, jnp.logical_and(m >= 7, m < 11), m >= 11

    def valid(ch):
        return jnp.logical_and(ch >= 0, ch < NCH)

    def up(ch, col, j):
        return w_all.at[ch, c, col, 0, pl.ds(j * 128, 128), :]

    def down(ch, col, j):
        return w_all.at[ch, c, col, 1, pl.ds((j // 2) * 256, 256), pl.ds((j % 2) * 128, 128)]

    def up2(ch, j):
        return w_all.at[ch, c, :, 0, pl.ds(j * 128, 128), :]

    def down2(ch, j):
        return w_all.at[ch, c, :, 1, pl.ds((j // 2) * 256, 256), pl.ds((j % 2) * 128, 128)]

    def one_band(ch):
        return w_all.at[ch, 0, 0, 0, pl.ds(0, 256), :]

    def two_bands(ch):
        return w_all.at[ch, 0, 0, 0]

    def unit(ch):
        return w_all.at[ch, 0, 0]

    def pair(ch):
        return w_all.at[ch, 0]

    @pl.when(side == 0)
    def _():
        def along(ch, j, right, su, sd, sem):
            dev = (t + 1, 0, r) if right else (t - 1, 0, r)
            send(su, up(ch, x, j), sem, b_sem.at[ch, j], dev)
            send(sd, down(ch, x, j), sem, b_sem.at[ch, j], dev)

        def across(ch, col, j, su, sd):
            send(su, up(ch, col, j), s1.at[ch], y_sem.at[ch], (t, 1, r))
            send(sd, down(ch, col, j), s1.at[ch], y_sem.at[ch], (t, 1, r))

        def slot(i, _):
            e = i - AHEAD
            chz = e + AHEAD
            is_a, is_b, is_g = kind(chz)
            f0 = pl.multiple_of(jnp.minimum(chz, NCH - 1) * FC, FC)
            su, sd = wu_in.at[:, pl.ds(f0, FC)], wd_in.at[pl.ds(f0, FC), :]

            @pl.when(jnp.logical_and(valid(chz), jnp.logical_not(is_a)))
            def _():
                across(chz, x, t, su, sd)

                @pl.when(is_g)
                def _():
                    send(su, up(chz, x, t), s2.at[chz], x_sem.at[chz], (t, 0, r ^ 2))
                    send(sd, down(chz, x, t), s2.at[chz], x_sem.at[chz], (t, 0, r ^ 2))

            cha = e
            is_a, _, _ = kind(cha)
            f1 = pl.multiple_of(jnp.maximum(jnp.minimum(cha, NCH - 1), 0) * FC, FC)
            su1, sd1 = wu_in.at[:, pl.ds(f1, FC)], wd_in.at[pl.ds(f1, FC), :]

            @pl.when(jnp.logical_and(valid(cha), is_a))
            def _():
                across(cha, x, t, su1, sd1)

                @pl.when(t < 3)
                def _():
                    along(cha, t, True, su1, sd1, sb.at[cha, t])

                @pl.when(t > 0)
                def _():
                    along(cha, t, False, su1, sd1, s3.at[cha])

            for k in (1, 2, 3):
                ch = e - k
                is_a, _, _ = kind(ch)
                go = jnp.logical_and(valid(ch), is_a)

                @pl.when(jnp.logical_and(go, t >= k))
                def _():
                    j = t - k
                    wait(one_band(ch), b_sem.at[ch, j])
                    across(ch, x, j, up(ch, x, j), down(ch, x, j))

                    @pl.when(t < 3)
                    def _():
                        along(ch, j, True, up(ch, x, j), down(ch, x, j), sb.at[ch, j])

                @pl.when(jnp.logical_and(go, t + k <= 3))
                def _():
                    j = t + k
                    wait(one_band(ch), b_sem.at[ch, j])
                    across(ch, x, j, up(ch, x, j), down(ch, x, j))

                    @pl.when(t > 0)
                    def _():
                        along(ch, j, False, up(ch, x, j), down(ch, x, j), sb.at[ch, j])

            chg = e + AHEAD - 1
            _, _, is_g = kind(chg)

            @pl.when(jnp.logical_and(valid(chg), is_g))
            def _():
                wait(one_band(chg), x_sem.at[chg])
                across(chg, 1 - x, t, up(chg, 1 - x, t), down(chg, 1 - x, t))

            return 0

        lax.fori_loop(0, NCH + AHEAD + 4, slot, 0)

        h[pl.ds(0, M), :] = jnp.zeros((M, D), BF)
        for i in range(TOK // M):
            pltpu.make_async_copy(h.at[pl.ds(0, M)], out.at[pl.ds(i * M, M)], o_sem).start()

        @pl.when(jnp.logical_or(t == 1, t == 2))
        def _():
            base = jnp.where(t == 1, R1, 0)
            end = jnp.where(t == 1, 0, 3)
            odd = t - 1

            def piece(i, _):
                wait(relay.at[i], r_recv.at[i])
                row = pl.multiple_of(base + (2 * i + odd) * PC, PC)
                send(relay.at[i], out.at[pl.ds(row, PC)], e_send.at[2], e_recv.at[odd], (end, 1, r))
                return 0

            lax.fori_loop(0, NPC // 2, piece, 0)
            wait(relay, e_send.at[2])

        def drain(ch, _):
            is_a, is_b, is_g = kind(ch)

            @pl.when(is_a)
            def _():
                wait(unit(ch), s1.at[ch])

                @pl.when(t > 0)
                def _():
                    wait(one_band(ch), s3.at[ch])

                for j in range(4):
                    hops = jnp.logical_or(
                        jnp.logical_and(j <= t, t < 3), jnp.logical_and(j > t, t > 0)
                    )

                    @pl.when(hops)
                    def _():
                        wait(one_band(ch), sb.at[ch, j])

            @pl.when(is_b)
            def _():
                wait(one_band(ch), s1.at[ch])

            @pl.when(is_g)
            def _():
                wait(two_bands(ch), s1.at[ch])
                wait(one_band(ch), s2.at[ch])

            return 0

        lax.fori_loop(0, NCH, drain, 0)
        wait(out, o_sem)

    @pl.when(side == 1)
    def _():
        sib, opp = (t, 1, r ^ 1), (t, 1, r ^ 2)
        base = jnp.where(t % 2 == 0, 0, R1)

        def over(ref, ch, dev):
            send(ref, ref, s1.at[ch], d_sem.at[ch], dev)

        def hop(ch, j, right, sem, is_b, is_g):
            dev = (t + 1, 1, r) if right else (t - 1, 1, r)

            @pl.when(is_b)
            def _():
                for ref in (up(ch, x, j), down(ch, x, j)):
                    send(ref, ref, sem, b_sem.at[ch, j], dev)

            @pl.when(is_g)
            def _():
                for ref in (up2(ch, j), down2(ch, j)):
                    send(ref, ref, sem, b_sem.at[ch, j], dev)

        def tick(e):
            is_a, _, _ = kind(e)
            own = w_all.at[e, c, x]

            @pl.when(jnp.logical_and(valid(e), is_a))
            def _():
                wait(unit(e), y_sem.at[e])
                send(own, own, s2.at[e], x_sem.at[e], opp)
                over(own, e, sib)

            ch = e + AHEAD
            is_a, is_b, is_g = kind(ch)

            @pl.when(jnp.logical_and(valid(ch), jnp.logical_not(is_a)))
            def _():
                @pl.when(is_b)
                def _():
                    wait(one_band(ch), y_sem.at[ch])

                @pl.when(is_g)
                def _():
                    wait(two_bands(ch), y_sem.at[ch])

                @pl.when(t < 3)
                def _():
                    hop(ch, t, True, sb.at[ch, t], is_b, is_g)

                @pl.when(t > 0)
                def _():
                    hop(ch, t, False, s3.at[ch], is_b, is_g)

            for k in (1, 2, 3):
                chk = e + AHEAD - k
                is_a, kb, kg = kind(chk)
                go = jnp.logical_and(valid(chk), jnp.logical_not(is_a))

                def arrive(j):
                    @pl.when(kb)
                    def _():
                        wait(one_band(chk), b_sem.at[chk, j])

                    @pl.when(kg)
                    def _():
                        wait(two_bands(chk), b_sem.at[chk, j])

                @pl.when(jnp.logical_and(go, t >= k))
                def _():
                    arrive(t - k)

                    @pl.when(t < 3)
                    def _():
                        hop(chk, t - k, True, sb.at[chk, t - k], kb, kg)

                @pl.when(jnp.logical_and(go, t + k <= 3))
                def _():
                    arrive(t + k)

                    @pl.when(t > 0)
                    def _():
                        hop(chk, t + k, False, sb.at[chk, t + k], kb, kg)

            ch3 = e + AHEAD - 3
            _, is_b, is_g = kind(ch3)

            @pl.when(jnp.logical_and(valid(ch3), is_b))
            def _():
                mine = w_all.at[ch3, c, x]
                send(mine, mine, s2.at[ch3], x_sem.at[ch3], opp)
                over(mine, ch3, sib)

            @pl.when(jnp.logical_and(valid(ch3), is_g))
            def _():
                over(w_all.at[ch3, c], ch3, sib)

            chx = e - LAGX
            _, _, is_g = kind(chx)

            @pl.when(jnp.logical_and(valid(chx), jnp.logical_not(is_g)))
            def _():
                wait(unit(chx), x_sem.at[chx])
                over(w_all.at[chx, c, 1 - x], chx, sib)

        def load(ch, slot, half, start):
            for cc in range(2):
                for xx in range(2):
                    d0 = (2 * xx + cc) * 512
                    cps = [
                        pltpu.make_async_copy(
                            w_all.at[ch, cc, xx, 0],
                            wu.at[slot, pl.ds(d0, 512), pl.ds(half * FC, FC)],
                            ld_sem.at[slot, half, 0],
                        )
                    ]
                    for q in range(2):
                        cps.append(
                            pltpu.make_async_copy(
                                w_all.at[ch, cc, xx, 1, pl.ds(q * 256, 256), :],
                                wd.at[slot, pl.ds(half * FC, FC), pl.ds(d0 + q * 256, 256)],
                                ld_sem.at[slot, half, 1],
                            )
                        )
                    for cp in cps:
                        cp.start()

        def loaded(slot, half):
            wait(wu.at[slot, :, pl.ds(half * FC, FC)], ld_sem.at[slot, half, 0])
            wait(wd.at[slot, pl.ds(half * FC, FC), :], ld_sem.at[slot, half, 1])

        def fetch(row, n, dst):
            return pltpu.make_async_copy(rows_in.at[pl.ds(row, n)], h.at[pl.ds(dst, n)], h_sem)

        def ready(ch):
            wait(pair(ch), d_sem.at[ch])

        first = fetch(pl.multiple_of(base, M), R1, 0)
        first.start()

        def zero(i, _):
            acc[pl.ds(pl.multiple_of(i * 256, 256), 256), :] = jnp.zeros((256, D), F32)
            return 0

        lax.fori_loop(0, R1 // 256, zero, 0)
        first.wait()

        e0 = LAGD + 2
        lax.fori_loop(-AHEAD, e0, lambda e, _: (tick(e), 0)[1], 0)
        for half in range(2):
            ready(half)
            load(half, 0, half, True)

        def give(i):
            @pl.when(i >= 0)
            def _():
                for q in range(M // PC):
                    p = i * (M // PC) + q
                    src = out.at[pl.ds(pl.multiple_of(base + p * PC, PC), PC)]
                    if q % 2 == 0:

                        @pl.when(t < 3)
                        def _():
                            send(src, src, e_send.at[0], e_recv.at[0], (t + 1, 1, r))

                        @pl.when(t == 1)
                        def _():
                            i2 = i * (M // PC // 2) + q // 2
                            send(src, relay.at[i2], e_send.at[2], r_recv.at[i2], (t, 0, r))
                    else:

                        @pl.when(t > 0)
                        def _():
                            send(src, src, e_send.at[1], e_recv.at[1], (t - 1, 1, r))

                        @pl.when(t == 2)
                        def _():
                            i2 = i * (M // PC // 2) + q // 2
                            send(src, relay.at[i2], e_send.at[2], r_recv.at[i2], (t, 0, r))

        def step(sp, _):
            pas, st, slot = sp // NST, sp % NST, sp % 2
            for half in range(2):
                loaded(slot, half)

            @pl.when(sp == NST)
            def _():
                wait(h.at[pl.ds(0, R2)], h_sem)

            def block(i, _):
                rs = pl.ds(pl.multiple_of(i * M, M), M)

                @pl.when(i < 2)
                def _():
                    n = 2 * (sp + 1) + i

                    @pl.when(n < NCH + 2)
                    def _():
                        tick(e0 + n - 2)

                    @pl.when(n < NCH)
                    def _():
                        ready(n)

                    @pl.when(n < 2 * NCH)
                    def _():
                        for half in range(2):

                            @pl.when(i == half)
                            def _():
                                load(n % NCH, 1 - slot, half, True)

                @pl.when(jnp.logical_and(sp == NST - 1, i > 0))
                def _():
                    wait(h.at[pl.ds(0, M)], o_sem)
                    give(i - 1)
                    j = pl.multiple_of((i - 1) * M, M)
                    fetch(2 * R1 + j, M, j).start()

                a = jnp.dot(h[rs, :], wu[slot], preferred_element_type=F32)
                u = gelu(a).astype(BF)
                for q in range(2):
                    cs = pl.ds(q * (D // 2), D // 2)
                    acc[rs, cs] += jnp.dot(u, wd[slot, :, cs], preferred_element_type=F32)

                @pl.when(st == NST - 1)
                def _():
                    def fin(q, _):
                        qs = pl.ds(pl.multiple_of(i * M + q * 128, 128), 128)
                        h[qs, :] = (h[qs, :].astype(F32) + acc[qs, :]).astype(BF)
                        acc[qs, :] = jnp.zeros((128, D), F32)
                        return 0

                    lax.fori_loop(0, M // 128, fin, 0)
                    row = pl.multiple_of(jnp.where(pas == 0, base, 2 * R1) + i * M, M)
                    pltpu.make_async_copy(h.at[rs], out.at[pl.ds(row, M)], o_sem).start()

                return 0

            lax.fori_loop(0, 3 - pas, block, 0)

            @pl.when(sp == NST - 1)
            def _():
                wait(h.at[pl.ds(0, M)], o_sem)
                give(R1 // M - 1)

            return 0

        lax.fori_loop(0, 2 * NST, step, 0)
        wait(h.at[pl.ds(0, R2)], o_sem)

        half_rows = out.at[pl.ds(0, R1 // 2)]
        wait(half_rows, e_recv.at[0])
        wait(half_rows, e_recv.at[1])

        @pl.when(t < 3)
        def _():
            wait(half_rows, e_send.at[0])

        @pl.when(t > 0)
        def _():
            wait(half_rows, e_send.at[1])

        @pl.when(jnp.logical_or(t == 1, t == 2))
        def _():
            wait(half_rows, e_send.at[2])

        def drain(ch, _):
            is_a, is_b, is_g = kind(ch)
            wait(pair(ch), s1.at[ch])

            @pl.when(jnp.logical_not(is_g))
            def _():
                wait(unit(ch), s2.at[ch])

            for size, on in ((one_band, is_b), (two_bands, is_g)):

                @pl.when(on)
                def _():
                    @pl.when(t > 0)
                    def _():
                        wait(size(ch), s3.at[ch])

                    for j in range(4):
                        hops = jnp.logical_or(
                            jnp.logical_and(j <= t, t < 3), jnp.logical_and(j > t, t > 0)
                        )

                        @pl.when(hops)
                        def _():
                            wait(size(ch), sb.at[ch, j])

            return 0

        lax.fori_loop(0, NCH, drain, 0)


def sync_and_run(wu, wd, rows):
    dma = pltpu.SemaphoreType.DMA
    any_ = pl.BlockSpec(memory_space=pl.ANY)
    out, _, _ = pl.pallas_call(
        kernel,
        out_shape=(
            jax.ShapeDtypeStruct((TOK, D), BF),
            jax.ShapeDtypeStruct((NCH, 2, 2, 2, 512, FC), BF),
            jax.ShapeDtypeStruct((NPC // 2, PC, D), BF),
        ),
        in_specs=[any_] * 3,
        out_specs=(any_,) * 3,
        scratch_shapes=[
            pltpu.VMEM((R1, D), BF),
            pltpu.VMEM((R1, D), F32),
            pltpu.VMEM((2, D, FS), BF),
            pltpu.VMEM((2, FS, D), BF),
            dma((NCH,)), dma((NCH,)), dma((NCH, 4)), dma((NCH,)),
            dma((NCH,)), dma((NCH,)), dma((NCH,)), dma((NCH, 4)),
            dma((2, 2, 2)), dma(()), dma(()), dma((2,)), dma((3,)), dma((NPC // 2,)),
        ],
        compiler_params=pltpu.CompilerParams(
            has_side_effects=True, vmem_limit_bytes=67043328
        ),
        name="sync_and_run",
    )(wu, wd, rows)
    return out


def solution(mesh):
    up_spec = P("side", None, ("rep", "tp"), None)
    down_spec = P("side", None, None, ("rep", "tp"))
    tok_spec = P("side", "rep", None, None)

    def device_step(w_up, w_down, g_up, g_down, learn_rate, prompts):
        rate = learn_rate[0]
        new_up = w_up - rate * g_up
        new_down = w_down - rate * g_down
        out = sync_and_run(new_up[0, 0].astype(BF), new_down[0, 0].astype(BF), prompts[0, 0])
        return new_up, new_down, out[None, None]

    return jax.shard_map(
        device_step,
        mesh=mesh,
        in_specs=(up_spec, down_spec, up_spec, down_spec, P("side"), tok_spec),
        out_specs=(up_spec, down_spec, tok_spec),
        check_vma=False,
    )
```

time: 2790 us -> 576 us (0.21)
  waiting for transfers between devices: 2280 us -> 0 us
  Pallas kernels: 0 us -> 541 us
  matrix products: 176 us -> 0 us
  other arithmetic: 145 us -> 10.3 us
  blocking collectives: 104 us -> 0 us
  local copies, waits for them, and re-layouts: 61.5 us -> 23.3 us
    psum x1 -> x0, waiting for transfers between devices: 2180 us -> none  [device_step(): part_sum = lax.psum(part_sum, 'tp')]
    pallas_call x0 -> x1, Pallas kernels: none -> 541 us  [sync_and_run(): pl.pallas_call(kernel, out_shape=(jax.ShapeDtypeStruct((TOK, D), BF), jax...]
    dot_general x2 -> x0, matrix products: 176 us -> none  [the longest x1 96.6 us: device_step(): jnp.dot(hidden, full_up[layer], preferred_element_type=jnp.float32)]
    all_to_all x2 -> x0, blocking collectives: 104 us -> none  [the longest x1 52.5 us: device_step(): band_up = lax.all_to_all(recv_up, 'tp', 2, 1, tiled=True)]
    ppermute x2 -> x0, waiting for transfers between devices: 95.3 us -> none  [the longest x1 48 us: device_step(): lax.ppermute(new_up[0].astype(jnp.bfloat16), 'side', perm=[(0, 1)])]
    unnamed x2 -> x0, other arithmetic: 90.2 us -> none
    broadcast_in_dim x1 -> x0, other arithmetic: 42.6 us -> none  [device_step(): return (new_up, new_down, gen_out[None, None])]
    ppermute x2 -> x0, local copies, waits for them, and re-layouts: 40 us -> none  [the longest x1 33.2 us: device_step(): lax.ppermute(new_down[0].astype(jnp.bfloat16), 'side', perm=[(0, 1)])]
  transfers between devices with their start and end apart: 5 -> 0, of which waited for: 3 -> 0; matrix products, arithmetic and copies ran while one was open for 7% -> 0% of each run, Pallas kernels for 0% -> 0%
where the time goes in v1:
time: 576 us; the launch traced here: 575 us
  Pallas kernels  541 us (94%)
  local copies, waits for them, and re-layouts  23.3 us (4%)
  other arithmetic  10.3 us (2%)
    pallas_call x1, Pallas kernels, sync_and_run(): pl.pallas_call(kernel, out_shape=(jax.ShapeDtypeStruct((TOK, D), BF), jax...  541 us
    unnamed x5, local copies, waits for them, and re-layouts  23.3 us

profile of v1, /device:TPU:4, one launch (start us, length us, event | category | flops | bytes accessed | tf_op | source)
XLA Modules:
  0.0 575.4 jit_solution(1649066856889306945)
XLA Ops:
  1.3 0.0 copy-start
  1.3 0.0 copy-start.1
  1.3 7.0 %convert_bitcast_fusion.1 = (bf16[128,8192]{1,0:T(8,128)(2,1)}, f32[1,1,128,8192]{3,2,1,0:T(8,128)}) fusion(f32[1,1,128,8192]{3,2,1,0:T(8,128)} %param.6, f32[1,1,128,8192]{3,2,1,0:T(8,128)} %param.8, f32[]{:T(128)} %bitcast.7), kind=kLoop, calls=%fused_computation.3 | loop fusion | flops 3145728 | bytes 14680068 | tf_op jit(solution)/shard_map/convert_element_type | solution.py:546
  8.3 0.0 copy-done
  8.3 0.4 copy-done.1
  8.7 3.3 convert_bitcast_fusion
  12.0 540.5 %sync_and_run.1 = (bf16[8192,2048]{1,0:T(8,128)(2,1)}, bf16[32,2,2,2,512,256]{5,4,3,2,1,0:T(8,128)(2,1)}, bf16[6,256,2048]{2,1,0:T(8,128)(2,1)}) custom-call(bf16[128,8192]{1,0:T(8,128)(2,1)} %get-tuple-element.7.wu_in, bf16[8192,128]{1,0:T(8,128)(2,1)} %get-tuple-element.5.wd_in, bf16[8192,2048]{1,0:T(8,128)(2,1)} %bitcast.9), custom_call_target="tpu_custom_call" | custom-call | tf_op jit(solution)/shard_map/sync_and_run/pallas_call | solution.py:511
  552.5 22.9 %copy.11 = bf16[1,1,8192,2048]{3,2,1,0:T(8,128)(2,1)} copy(bf16[1,1,8192,2048]{3,2,1,0:T(8,128)(2,1)} %bitcast.10) | data formatting | bytes 67108864
Async XLA Ops:
  1.3 7.1 %copy-start = (f32[1,1,8192,128]{3,2,1,0:T(8,128)S(1)}, f32[1,1,8192,128]{3,2,1,0:T(8,128)}, u32[]{:S(2)}) copy-start(f32[1,1,8192,128]{3,2,1,0:T(8,128)} %param.7) | copy-start | bytes 12582916
  1.3 7.4 %copy-start.1 = (f32[1,1,8192,128]{3,2,1,0:T(8,128)S(1)}, f32[1,1,8192,128]{3,2,1,0:T(8,128)}, u32[]{:S(2)}) copy-start(f32[1,1,8192,128]{3,2,1,0:T(8,128)} %param.9) | copy-start | bytes 12582916

commit v2 on v0

v2 whole, which is shorter than its diff:
```python
import functools
import math

import jax
import jax.numpy as jnp
from jax import lax
from jax.experimental import pallas as pl
from jax.experimental.pallas import tpu as pltpu
from jax.sharding import PartitionSpec as P

BF, F32 = jnp.bfloat16, jnp.float32
MESH = pl.DeviceIdType.MESH
D, F, TOK = 2048, 8192, 8192
FC = 128
NCH = F // FC
QS = 4
NST = NCH // QS
M1 = 768
R1 = QS * M1
R2 = TOK - 2 * R1
M2 = R2 // 2
PC = 128
NPC = R1 // PC
N_A, N_B, MUL, OFF = 30, 14, 19, 2
N_G = NCH - N_A - N_B
B0 = 8


def gelu(a):
    k = math.sqrt(2.0 / math.pi)
    half = 0.5 * a
    return half + half * jnp.tanh(a * (k + (k * 0.044715) * (a * a)))


def reached(b):
    n, left = b + B0, jnp.maximum(0, NCH - 5 - b)

    def lead(most, at_first):
        return jnp.minimum(most, jnp.minimum(at_first + lax.div(3 * jnp.maximum(n, 0), 2), 2 * left))

    x = lead(1, 1)
    h3 = jnp.maximum(x, lead(3, 3))
    h2 = jnp.maximum(h3, lead(5, 4))
    h1 = jnp.maximum(h2, lead(7, 5))
    yz = jnp.maximum(h1, lead(9, 6))
    ya = jnp.maximum(x, lead(4, 2))
    return [
        jnp.where(n < 0, 0, jnp.clip(b + 5 + v, 0, NCH)) for v in (ya, yz, h1, h2, h3, x, 0)
    ]


def spans(b):
    return list(zip(reached(b - 1), reached(b)))


def each(span, body):
    lax.fori_loop(span[0], span[1], lambda ch, _: (body(ch), 0)[1], 0)


def kernel(
    rate, wu_in, gu_in, wd_in, gd_in, rows_in, out, w_all, relay, h, h2, acc, wv,
    y_sem, x_sem, b_sem, d_sem, s_over, s_opp, s_y, s_z, ld_sem, up_sem, h_sem, o_sem,
    e_recv, e_send, r_recv,
):
    t, side, r = lax.axis_index("tp"), lax.axis_index("side"), lax.axis_index("rep")
    x, c = r // 2, r % 2

    def send(src, dst, send_sem, recv_sem, device):
        pltpu.make_async_remote_copy(
            src, dst, send_sem, recv_sem, device_id=device, device_id_type=MESH
        ).start()

    def wait(ref, sem):
        pltpu.make_async_copy(ref, ref, sem).wait()

    def kind(ch):
        m = lax.rem((ch + OFF) * MUL, NCH)
        return m < N_A, jnp.logical_and(m >= N_A, m < N_A + N_B), m >= N_A + N_B

    def band(ch, col, j):
        return w_all.at[ch, c, col, :, pl.ds(j * 128, 128), :]

    def band2(ch, j):
        return w_all.at[ch, c, :, :, pl.ds(j * 128, 128), :]

    def amount(n):
        if n % 16 == 0:
            return w_all.at[pl.ds(0, n // 16)]
        if n % 8 == 0:
            return w_all.at[pl.ds(0, n // 8), 0]
        if n % 4 == 0:
            return w_all.at[pl.ds(0, n // 4), 0, 0]
        if n % 2 == 0:
            return w_all.at[pl.ds(0, n // 2), 0, 0, 0]
        return w_all.at[pl.ds(0, n), 0, 0, 0, pl.ds(0, 256), :]

    @pl.when(side == 0)
    def _():
        def parts(g):
            s = g % 2
            f0 = pl.multiple_of(g * QS * FC, QS * FC)
            cols, rows = pl.ds(f0, QS * FC), pl.ds(f0, QS * FC)
            up, dn = pl.ds(128 * s, 128), pl.ds(512 + 512 * s, 512)
            return [
                pltpu.make_async_copy(src, dst, up_sem.at[s, k])
                for k, (src, dst) in enumerate(
                    (
                        (wu_in.at[:, cols], acc.at[up, pl.ds(0, 512)]),
                        (gu_in.at[:, cols], acc.at[up, pl.ds(512, 512)]),
                        (wd_in.at[rows, :], acc.at[dn, pl.ds(0, 128)]),
                        (gd_in.at[rows, :], acc.at[dn, pl.ds(128, 128)]),
                    )
                )
            ]

        def update(g):
            s = g % 2
            for cp in parts(g):
                cp.wait()

            @pl.when(g + 1 < NST)
            def _():
                for cp in parts(g + 1):
                    cp.start()

            lr = rate[0]
            up = pl.ds(pl.multiple_of(128 * s, 128), 128)
            new_up = (acc[up, 0:512] - lr * acc[up, 512:1024]).astype(BF)
            for q in range(QS):
                wv[QS * s + q, 0, 0, 0, 0:128, :] = new_up[:, q * FC : (q + 1) * FC]
                dn = pl.ds(pl.multiple_of(512 + 512 * s + q * FC, FC), FC)
                new_dn = (acc[dn, 0:128] - lr * acc[dn, 128:256]).astype(BF)
                wv[QS * s + q, 0, 0, 1, 0:128, :] = new_dn
            cp = pltpu.make_async_copy(
                wv.at[pl.ds(QS * s, QS), 0, 0, :, pl.ds(0, 128), :],
                w_all.at[pl.ds(QS * g, QS), c, x, :, pl.ds(t * 128, 128), :],
                o_sem,
            )
            cp.start()
            cp.wait()

        def along(ch, j, right):
            if right:
                send(band(ch, x, j), band(ch, x, j), s_z.at[0, 0], b_sem.at[ch, j], (t + 1, 0, r))
            else:
                send(band(ch, x, j), band(ch, x, j), s_z.at[1, 0], b_sem.at[ch, j], (t - 1, 0, r))

        def across(ch, col, j, k):
            send(band(ch, col, j), band(ch, col, j), s_y.at[k], y_sem.at[ch], (t, 1, r))

        def own_a(ch):
            @pl.when(kind(ch)[0])
            def _():
                across(ch, x, t, 0)

                @pl.when(t < 3)
                def _():
                    along(ch, t, True)

                @pl.when(t > 0)
                def _():
                    along(ch, t, False)

        def own_z(ch):
            is_a, _, is_g = kind(ch)

            @pl.when(jnp.logical_not(is_a))
            def _():
                across(ch, x, t, 1)

            @pl.when(is_g)
            def _():
                send(band(ch, x, t), band(ch, x, t), s_opp, x_sem.at[ch], (t, 0, r ^ 2))

        def from_opp(ch):
            @pl.when(kind(ch)[2])
            def _():
                wait(amount(1), x_sem.at[ch])
                across(ch, 1 - x, t, 1)

        def hop(k):
            def body(ch):
                is_a = kind(ch)[0]

                @pl.when(jnp.logical_and(is_a, t >= k))
                def _():
                    wait(amount(1), b_sem.at[ch, t - k])
                    across(ch, x, t - k, 0)

                    @pl.when(t < 3)
                    def _():
                        along(ch, t - k, True)

                @pl.when(jnp.logical_and(is_a, t + k <= 3))
                def _():
                    wait(amount(1), b_sem.at[ch, t + k])
                    across(ch, x, t + k, 0)

                    @pl.when(t > 0)
                    def _():
                        along(ch, t + k, False)

            return body

        for cp in parts(0):
            cp.start()

        def slot(b, done):
            ya, yz = spans(b)[:2]
            todo = (jnp.maximum(ya[1], yz[1]) + QS - 1) // QS
            each((done, todo), update)
            each(ya, own_a)
            each(yz, own_z)

            @pl.when(b == -B0)
            def _():
                for k in (1, 2, 3):
                    each(ya, hop(k))

            for k in (1, 2, 3):
                lo, hi = spans(b - k)[0]
                each((lo, jnp.where(b - k > -B0, hi, lo)), hop(k))
            each(yz, from_opp)
            return todo

        lax.fori_loop(-B0, NCH + 4, slot, 0)

        @pl.when(jnp.logical_or(t == 1, t == 2))
        def _():
            base = jnp.where(t == 1, R1, 0)
            end = jnp.where(t == 1, 0, 3)
            odd = t - 1

            def piece(i, _):
                wait(relay.at[i], r_recv.at[i])
                row = pl.multiple_of(base + (2 * i + odd) * PC, PC)
                send(relay.at[i], out.at[pl.ds(row, PC)], e_send.at[2], e_recv.at[odd], (end, 1, r))
                return 0

            lax.fori_loop(0, NPC // 2, piece, 0)
            wait(relay, e_send.at[2])

        wait(amount(4 * N_A), s_y.at[0])
        wait(amount(N_B + 2 * N_G), s_y.at[1])
        wait(amount(N_G), s_opp)
        for tt in range(4):

            @pl.when(t == tt)
            def _():
                if tt < 3:
                    wait(amount((tt + 1) * N_A), s_z.at[0, 0])
                if tt > 0:
                    wait(amount((4 - tt) * N_A), s_z.at[1, 0])


    @pl.when(side == 1)
    def _():
        sib, opp = (t, 1, r ^ 1), (t, 1, r ^ 2)
        base = jnp.where(t % 2 == 0, 0, R1)

        def over(ref, ch):
            send(ref, ref, s_over, d_sem.at[ch], sib)

        def along(ch, j, right, is_b, is_g):
            k = 0 if right else 1
            dev = (t + 1, 1, r) if right else (t - 1, 1, r)

            @pl.when(is_b)
            def _():
                send(band(ch, x, j), band(ch, x, j), s_z.at[k, 0], b_sem.at[ch, j], dev)

            @pl.when(is_g)
            def _():
                send(band2(ch, j), band2(ch, j), s_z.at[k, 1], b_sem.at[ch, j], dev)

        def arrive(sem, is_b, is_g):
            @pl.when(is_b)
            def _():
                wait(amount(1), sem)

            @pl.when(is_g)
            def _():
                wait(amount(2), sem)

        def across(ch):
            own = w_all.at[ch, c, x]
            send(own, own, s_opp, x_sem.at[ch], opp)
            over(own, ch)

        def ya(ch):
            @pl.when(kind(ch)[0])
            def _():
                wait(amount(4), y_sem.at[ch])
                across(ch)

        def yz(ch):
            is_a, is_b, is_g = kind(ch)

            @pl.when(jnp.logical_not(is_a))
            def _():
                arrive(y_sem.at[ch], is_b, is_g)

                @pl.when(t < 3)
                def _():
                    along(ch, t, True, is_b, is_g)

                @pl.when(t > 0)
                def _():
                    along(ch, t, False, is_b, is_g)

        def hop(k):
            def body(ch):
                is_a, is_b, is_g = kind(ch)

                @pl.when(jnp.logical_and(jnp.logical_not(is_a), t >= k))
                def _():
                    arrive(b_sem.at[ch, t - k], is_b, is_g)

                    @pl.when(t < 3)
                    def _():
                        along(ch, t - k, True, is_b, is_g)

                @pl.when(jnp.logical_and(jnp.logical_not(is_a), t + k <= 3))
                def _():
                    arrive(b_sem.at[ch, t + k], is_b, is_g)

                    @pl.when(t > 0)
                    def _():
                        along(ch, t + k, False, is_b, is_g)

                if k == 3:

                    @pl.when(is_b)
                    def _():
                        across(ch)

                    @pl.when(is_g)
                    def _():
                        over(w_all.at[ch, c], ch)

            return body

        def from_opp(ch):
            @pl.when(jnp.logical_not(kind(ch)[2]))
            def _():
                wait(amount(4), x_sem.at[ch])
                over(w_all.at[ch, c, 1 - x], ch)

        def load(ch, ring):
            pltpu.make_async_copy(w_all.at[ch], wv.at[ring], ld_sem.at[ring]).start()

        def ready(ch):
            wait(amount(8), d_sem.at[ch])
            load(ch, ch % (2 * QS))

        def tick(b):
            stages = (ya, yz, hop(1), hop(2), hop(3), from_opp, ready)
            for span, stage in zip(spans(b), stages):
                each(span, stage)

        def loaded(slot):
            for q in range(QS):
                wait(wv.at[QS * slot + q], ld_sem.at[QS * slot + q])

        def store(ref, row, n, to):
            return pltpu.make_async_copy(ref.at[pl.ds(row, n)], out.at[pl.ds(to, n)], o_sem)

        first = pltpu.make_async_copy(
            rows_in.at[pl.ds(pl.multiple_of(base, 1024), R1)], h, h_sem.at[0]
        )
        second = pltpu.make_async_copy(rows_in.at[pl.ds(2 * R1, R2)], h2, h_sem.at[1])
        first.start()
        second.start()

        def zero(i, _):
            acc[pl.ds(pl.multiple_of(i * 128, 128), 128), :] = jnp.zeros((128, D), F32)
            return 0

        lax.fori_loop(0, R1 // 128, zero, 0)
        first.wait()
        lax.fori_loop(-B0, 0, lambda b, _: (tick(b), 0)[1], 0)

        def give(i):
            for q in range(M1 // PC):
                p = i * (M1 // PC) + q
                src = out.at[pl.ds(pl.multiple_of(base + p * PC, PC), PC)]
                i2 = i * (M1 // PC // 2) + q // 2
                if q % 2 == 0:

                    @pl.when(t < 3)
                    def _():
                        send(src, src, e_send.at[0], e_recv.at[0], (t + 1, 1, r))

                    @pl.when(t == 1)
                    def _():
                        send(src, relay.at[i2], e_send.at[2], r_recv.at[i2], (t, 0, r))
                else:

                    @pl.when(t > 0)
                    def _():
                        send(src, src, e_send.at[1], e_recv.at[1], (t - 1, 1, r))

                    @pl.when(t == 2)
                    def _():
                        send(src, relay.at[i2], e_send.at[2], r_recv.at[i2], (t, 0, r))

        def multiply(ref, row, m, slot, first=False, last=False):
            rs = pl.ds(row, m)
            up = jnp.concatenate(
                [
                    jnp.concatenate([wv[QS * slot + q, k % 2, k // 2, 0] for q in range(QS)], axis=1)
                    for k in range(4)
                ],
                axis=0,
            )
            u = gelu(jnp.dot(ref[rs, :], up, preferred_element_type=F32)).astype(BF)
            for k in range(4):
                down = jnp.concatenate(
                    [
                        jnp.concatenate(
                            [
                                wv[QS * slot + q, k % 2, k // 2, 1, j * 128 : (j + 1) * 128, :]
                                for q in range(QS)
                            ],
                            axis=0,
                        )
                        for j in range(4)
                    ],
                    axis=1,
                )
                cs = pl.ds(k * 512, 512)
                part = jnp.dot(u, down, preferred_element_type=F32)
                if last:
                    ref[rs, cs] = (ref[rs, cs].astype(F32) + (acc[rs, cs] + part)).astype(BF)
                elif first:
                    acc[rs, cs] = part
                else:
                    acc[rs, cs] += part

        def step1(sp, _):
            slot = lax.rem(sp, 2)
            loaded(slot)

            def block(i, _):
                row = pl.multiple_of(i * M1, M1)
                tick(QS * sp + i)

                @pl.when(sp < NST - 1)
                def _():
                    multiply(h, row, M1, slot)

                @pl.when(sp == NST - 1)
                def _():
                    load(i, i)

                    @pl.when(i > 0)
                    def _():
                        wait(h.at[pl.ds(0, M1)], o_sem)
                        give(i - 1)

                    multiply(h, row, M1, slot, last=True)
                    store(h, row, M1, pl.multiple_of(base + i * M1, M1)).start()

                return 0

            lax.fori_loop(0, R1 // M1, block, 0)
            return 0

        lax.fori_loop(0, NST, step1, 0)
        second.wait()
        loaded(0)
        for q in range(QS):
            load(QS + q, QS + q)
        for i in range(R2 // M2):
            multiply(h2, i * M2, M2, 0, first=True)
            if i == 0:
                wait(h.at[pl.ds(0, M1)], o_sem)
                give(R1 // M1 - 1)

        def step2(sp, _):
            slot = lax.rem(sp, 2)
            loaded(slot)

            @pl.when(sp < NST - 1)
            def _():
                for q in range(QS):
                    load(QS * (sp + 1) + q, QS * (1 - slot) + q)

            def block(i, _):
                row = pl.multiple_of(i * M2, M2)

                @pl.when(sp < NST - 1)
                def _():
                    multiply(h2, row, M2, slot)

                @pl.when(sp == NST - 1)
                def _():
                    multiply(h2, row, M2, slot, last=True)
                    store(h2, row, M2, pl.multiple_of(2 * R1 + i * M2, M2)).start()

                return 0

            lax.fori_loop(0, R2 // M2, block, 0)
            return 0

        lax.fori_loop(1, NST, step2, 0)
        wait(h2, o_sem)

        half_rows = out.at[pl.ds(0, R1 // 2)]
        wait(half_rows, e_recv.at[0])
        wait(half_rows, e_recv.at[1])

        @pl.when(t < 3)
        def _():
            wait(half_rows, e_send.at[0])

        @pl.when(t > 0)
        def _():
            wait(half_rows, e_send.at[1])

        @pl.when(jnp.logical_or(t == 1, t == 2))
        def _():
            wait(half_rows, e_send.at[2])

        wait(amount(8 * NCH), s_over)
        wait(amount(4 * (N_A + N_B)), s_opp)
        for tt in range(4):

            @pl.when(t == tt)
            def _():
                if tt < 3:
                    wait(amount((tt + 1) * N_B), s_z.at[0, 0])
                    wait(amount((tt + 1) * 2 * N_G), s_z.at[0, 1])
                if tt > 0:
                    wait(amount((4 - tt) * N_B), s_z.at[1, 0])
                    wait(amount((4 - tt) * 2 * N_G), s_z.at[1, 1])


CR, RING = 512, 8


def finalize_kernel(
    rate, wu_in, gu_in, wd_in, gd_in, res, up_out, dn_out, out, buf, zero, zt, ub, un, r_sem, w_sem, u_sem, v_sem
):
    side = lax.axis_index("side")

    def copy(src, dst, sem):
        return pltpu.make_async_copy(src, dst, sem)

    @pl.when(side == 1)
    def _():
        def read(i):
            return copy(res.at[pl.ds(i * CR, CR)], buf.at[i % RING], r_sem.at[i % RING])

        def write(i):
            return copy(buf.at[i % RING], out.at[pl.ds(i * CR, CR)], w_sem.at[i % RING])

        n = TOK // CR
        for i in range(RING // 2):
            read(i).start()
        zero[...] = jnp.zeros_like(zero)
        for i in range(8):
            copy(zero.at[pl.ds(0, 128)], up_out.at[:, pl.ds(i * 1024, 1024)], u_sem.at[0, 0]).start()
            copy(zero.at[:, pl.ds(0, 128)], dn_out.at[pl.ds(i * 1024, 1024)], u_sem.at[0, 1]).start()
        for i in range(n):
            if i + RING // 2 < n:
                if i >= RING // 2:
                    write(i - RING // 2).wait()
                read(i + RING // 2).start()
            read(i).wait()
            write(i).start()
        for i in range(n - RING, n):
            write(i).wait()
        copy(up_out, up_out, u_sem.at[0, 0]).wait()
        copy(dn_out, dn_out, u_sem.at[0, 1]).wait()

    @pl.when(side == 0)
    def _():
        w = QS * FC

        def parts(g, s):
            f = pl.ds(pl.multiple_of(g * w, w), w)
            return (
                copy(wu_in.at[:, f], ub.at[s, 0], u_sem.at[s, 0]),
                copy(gu_in.at[:, f], ub.at[s, 1], u_sem.at[s, 1]),
                copy(wd_in.at[f, :], un.at[s, 0], u_sem.at[s, 2]),
                copy(gd_in.at[f, :], un.at[s, 1], u_sem.at[s, 3]),
            )

        def back(g, s):
            f = pl.ds(pl.multiple_of(g * w, w), w)
            return (
                copy(ub.at[s, 2], up_out.at[:, f], v_sem.at[s, 0]),
                copy(un.at[s, 2], dn_out.at[f, :], v_sem.at[s, 1]),
            )

        for cp in parts(0, 0) + parts(1, 1):
            cp.start()
        zt[...] = jnp.zeros_like(zt)
        for i in range(TOK // CR):
            copy(zt, out.at[pl.ds(i * CR, CR)], w_sem.at[0]).start()
        lr = rate[0]

        def group(g, _):
            s = lax.rem(g, 2)
            for cp in parts(g, s):
                cp.wait()

            @pl.when(g >= 2)
            def _():
                for cp in back(g - 2, s):
                    cp.wait()

            ub[s, 2] = ub[s, 0] - lr * ub[s, 1]
            un[s, 2] = un[s, 0] - lr * un[s, 1]
            for cp in back(g, s):
                cp.start()

            @pl.when(g + 2 < NST)
            def _():
                for cp in parts(g + 2, s):
                    cp.start()

            return 0

        lax.fori_loop(0, NST, group, 0)
        for s in range(2):
            for cp in back(NST - 2 + s, s):
                cp.wait()
        copy(out, out, w_sem.at[0]).wait()


def finalize(rate, wu, gu, wd, gd, res):
    dma = pltpu.SemaphoreType.DMA
    any_ = pl.BlockSpec(memory_space=pl.ANY)
    return pl.pallas_call(
        finalize_kernel,
        out_shape=(
            jax.ShapeDtypeStruct((128, F), F32),
            jax.ShapeDtypeStruct((F, 128), F32),
            jax.ShapeDtypeStruct((TOK, D), BF),
        ),
        in_specs=[pl.BlockSpec(memory_space=pltpu.SMEM)] + [any_] * 5,
        out_specs=(any_,) * 3,
        scratch_shapes=[
            pltpu.VMEM((RING, CR, D), BF),
            pltpu.VMEM((1024, 1024), F32),
            pltpu.VMEM((CR, D), BF),
            pltpu.VMEM((2, 3, 128, QS * FC), F32),
            pltpu.VMEM((2, 3, QS * FC, 128), F32),
            dma((RING,)), dma((RING,)), dma((2, 4)), dma((2, 2)),
        ],
        compiler_params=pltpu.CompilerParams(vmem_limit_bytes=60 << 20),
        name="finalize",
    )(rate, wu, gu, wd, gd, res)


def sync_and_run(rate, wu, gu, wd, gd, rows):
    dma = pltpu.SemaphoreType.DMA
    any_ = pl.BlockSpec(memory_space=pl.ANY)
    out, _, _ = pl.pallas_call(
        kernel,
        out_shape=(
            jax.ShapeDtypeStruct((TOK, D), BF),
            jax.ShapeDtypeStruct((NCH, 2, 2, 2, 512, FC), BF),
            jax.ShapeDtypeStruct((NPC // 2, PC, D), BF),
        ),
        in_specs=[pl.BlockSpec(memory_space=pltpu.SMEM)] + [any_] * 5,
        out_specs=(any_,) * 3,
        scratch_shapes=[
            pltpu.VMEM((R1, D), BF),
            pltpu.VMEM((R2, D), BF),
            pltpu.VMEM((R1, D), F32),
            pltpu.VMEM((2 * QS, 2, 2, 2, 512, FC), BF),
            dma((NCH,)), dma((NCH,)), dma((NCH, 4)), dma((NCH,)),
            dma(()), dma(()), dma((2,)), dma((2, 2)),
            dma((2 * QS,)), dma((2, 4)), dma((2,)), dma(()),
            dma((2,)), dma((3,)), dma((NPC // 2,)),
        ],
        compiler_params=pltpu.CompilerParams(
            has_side_effects=True, vmem_limit_bytes=67043328
        ),
        name="sync_and_run",
    )(rate, wu, gu, wd, gd, rows)
    return out


def solution(mesh):
    up_spec = P("side", None, ("rep", "tp"), None)
    down_spec = P("side", None, None, ("rep", "tp"))
    tok_spec = P("side", "rep", None, None)

    def device_step(w_up, w_down, g_up, g_down, learn_rate, prompts):
        weights = (learn_rate, w_up[0, 0], g_up[0, 0], w_down[0, 0], g_down[0, 0])
        res = sync_and_run(*weights, prompts[0, 0])
        new_up, new_down, out = finalize(*weights, res)
        return new_up[None, None], new_down[None, None], out[None, None]

    return jax.shard_map(
        device_step,
        mesh=mesh,
        in_specs=(up_spec, down_spec, up_spec, down_spec, P("side"), tok_spec),
        out_specs=(up_spec, down_spec, tok_spec),
        check_vma=False,
    )
```

time: 2790 us -> 500 us (0.18)
  waiting for transfers between devices: 2280 us -> 0 us
  Pallas kernels: 0 us -> 498 us
  matrix products: 176 us -> 0 us
  other arithmetic: 145 us -> 0 us
  blocking collectives: 104 us -> 0 us
  local copies, waits for them, and re-layouts: 61.5 us -> 0 us
    psum x1 -> x0, waiting for transfers between devices: 2180 us -> none  [device_step(): part_sum = lax.psum(part_sum, 'tp')]
    pallas_call x0 -> x2, Pallas kernels: none -> 498 us  [the longest x1 472 us: sync_and_run(): pl.pallas_call(kernel, out_shape=(jax.ShapeDtypeStruct((TOK, D), BF), jax...]
    dot_general x2 -> x0, matrix products: 176 us -> none  [the longest x1 96.6 us: device_step(): jnp.dot(hidden, full_up[layer], preferred_element_type=jnp.float32)]
    all_to_all x2 -> x0, blocking collectives: 104 us -> none  [the longest x1 52.5 us: device_step(): band_up = lax.all_to_all(recv_up, 'tp', 2, 1, tiled=True)]
    ppermute x2 -> x0, waiting for transfers between devices: 95.3 us -> none  [the longest x1 48 us: device_step(): lax.ppermute(new_up[0].astype(jnp.bfloat16), 'side', perm=[(0, 1)])]
    unnamed x2 -> x0, other arithmetic: 90.2 us -> none
    broadcast_in_dim x1 -> x0, other arithmetic: 42.6 us -> none  [device_step(): return (new_up, new_down, gen_out[None, None])]
    ppermute x2 -> x0, local copies, waits for them, and re-layouts: 40 us -> none  [the longest x1 33.2 us: device_step(): lax.ppermute(new_down[0].astype(jnp.bfloat16), 'side', perm=[(0, 1)])]
  transfers between devices with their start and end apart: 5 -> 0, of which waited for: 3 -> 0; matrix products, arithmetic and copies ran while one was open for 7% -> 0% of each run, Pallas kernels for 0% -> 0%
where the time goes in v2:
time: 500 us
  Pallas kernels  498 us (100%)
    pallas_call x1, Pallas kernels, sync_and_run(): pl.pallas_call(kernel, out_shape=(jax.ShapeDtypeStruct((TOK, D), BF), jax...  472 us
    pallas_call x1, Pallas kernels, finalize(): pl.pallas_call(finalize_kernel, out_shape=(jax.ShapeDtypeStruct((128, F),...  26 us

profile of v2, /device:TPU:4, one launch (start us, length us, event | category | flops | bytes accessed | tf_op | source)
XLA Modules:
  0.0 499.5 jit_solution(10086323532363140142)
XLA Ops:
  1.3 472.0 %sync_and_run.1 = (bf16[8192,2048]{1,0:T(8,128)(2,1)}, bf16[64,2,2,2,512,128]{5,4,3,2,1,0:T(8,128)(2,1)}, bf16[12,128,2048]{2,1,0:T(8,128)(2,1)}) custom-call(f32[1]{0:T(128)S(6)} %copy.9.rate, f32[128,8192]{1,0:T(8,128)} %bitcast.9, f32[128,8192]{1,0:T(8,128)} %bitcast.11, f32[8192,128]{1,0:T(8,128)} %bitcast.13, f32[8192,128]{1,0:T(8,128)} %bitcast.15, ...), custom_call_target="tpu_custom_call" | custom-call | tf_op jit(solution)/shard_map/sync_and_run/pallas_call | solution.py:661
  473.3 26.0 %finalize.1 = (f32[128,8192]{1,0:T(8,128)}, f32[8192,128]{1,0:T(8,128)}, bf16[8192,2048]{1,0:T(8,128)(2,1)}) custom-call(f32[1]{0:T(128)S(6)} %copy.9.rate, f32[128,8192]{1,0:T(8,128)} %bitcast.10, f32[128,8192]{1,0:T(8,128)} %bitcast.12, f32[8192,128]{1,0:T(8,128)} %bitcast.14, f32[8192,128]{1,0:T(8,128)} %bitcast.16, bf16[8192,2048]{1,0:T(8,128)(2,1)} %get-tuple-element.7.res), custom_call_target="tpu_custom_call" | custom-call | tf_op jit(solution)/shard_map/finalize/pallas_call | solution.py:636

commit v3 on v2

--- a/solution.py
+++ b/solution.py
@@ -15,46 +15,23 @@
 NCH = F // FC
 QS = 4
 NST = NCH // QS
-M1 = 768
+M1 = 800
 R1 = QS * M1
 R2 = TOK - 2 * R1
 M2 = R2 // 2
-PC = 128
+PC = 80
 NPC = R1 // PC
-N_A, N_B, MUL, OFF = 30, 14, 19, 2
+N_A, N_B, MUL, OFF = 29, 12, 23, 17
 N_G = NCH - N_A - N_B
-B0 = 8
+LEAD = 13
+YA, YZ, HOPS, OPP, DONE = 5, 0, (2, 4, 6), 8, 9
+T_AHEAD = 3
 
 
 def gelu(a):
     k = math.sqrt(2.0 / math.pi)
     half = 0.5 * a
     return half + half * jnp.tanh(a * (k + (k * 0.044715) * (a * a)))
-
-
-def reached(b):
-    n, left = b + B0, jnp.maximum(0, NCH - 5 - b)
-
-    def lead(most, at_first):
-        return jnp.minimum(most, jnp.minimum(at_first + lax.div(3 * jnp.maximum(n, 0), 2), 2 * left))
-
-    x = lead(1, 1)
-    h3 = jnp.maximum(x, lead(3, 3))
-    h2 = jnp.maximum(h3, lead(5, 4))
-    h1 = jnp.maximum(h2, lead(7, 5))
-    yz = jnp.maximum(h1, lead(9, 6))
-    ya = jnp.maximum(x, lead(4, 2))
-    return [
-        jnp.where(n < 0, 0, jnp.clip(b + 5 + v, 0, NCH)) for v in (ya, yz, h1, h2, h3, x, 0)
-    ]
-
-
-def spans(b):
-    return list(zip(reached(b - 1), reached(b)))
-
-
-def each(span, body):
-    lax.fori_loop(span[0], span[1], lambda ch, _: (body(ch), 0)[1], 0)
 
 
 def kernel(
@@ -73,9 +50,14 @@
     def wait(ref, sem):
         pltpu.make_async_copy(ref, ref, sem).wait()
 
-    def kind(ch):
+    def kind(i, late):
+        ch = jnp.clip(i - late, 0, NCH - 1)
+        real = jnp.logical_and(i >= late, i < NCH + late)
         m = lax.rem((ch + OFF) * MUL, NCH)
-        return m < N_A, jnp.logical_and(m >= N_A, m < N_A + N_B), m >= N_A + N_B
+        is_a = jnp.logical_and(real, m < N_A)
+        is_g = jnp.logical_and(real, m >= N_A + N_B)
+        not_a = jnp.logical_and(real, m >= N_A)
+        return ch, is_a, jnp.logical_and(not_a, m < N_A + N_B), is_g, not_a
 
     def band(ch, col, j):
         return w_all.at[ch, c, col, :, pl.ds(j * 128, 128), :]
@@ -84,18 +66,35 @@
         return w_all.at[ch, c, :, :, pl.ds(j * 128, 128), :]
 
     def amount(n):
-        if n % 16 == 0:
-            return w_all.at[pl.ds(0, n // 16)]
-        if n % 8 == 0:
-            return w_all.at[pl.ds(0, n // 8), 0]
-        if n % 4 == 0:
-            return w_all.at[pl.ds(0, n // 4), 0, 0]
-        if n % 2 == 0:
-            return w_all.at[pl.ds(0, n // 2), 0, 0, 0]
-        return w_all.at[pl.ds(0, n), 0, 0, 0, pl.ds(0, 256), :]
+        return out.at[pl.ds(0, 16 * n)]
+
+    barrier = pltpu.get_barrier_semaphore()
+
+    def greet(device):
+        pl.semaphore_signal(barrier, inc=1, device_id=device, device_id_type=MESH)
+
+    def greet_all(me):
+        greet((t, 1 - me, r))
+        greet((t, me, r ^ 2))
+
+        @pl.when(t < 3)
+        def _():
+            greet((t + 1, me, r))
+
+        @pl.when(t > 0)
+        def _():
+            greet((t - 1, me, r))
+
+        for relay_t, end_t in ((1, 0), (2, 3)):
+
+            @pl.when(t == (end_t if me else relay_t))
+            def _():
+                greet((relay_t if me else end_t, 1 - me, r))
 
     @pl.when(side == 0)
     def _():
+        greet_all(0)
+
         def parts(g):
             s = g % 2
             f0 = pl.multiple_of(g * QS * FC, QS * FC)
@@ -148,8 +147,10 @@
         def across(ch, col, j, k):
             send(band(ch, col, j), band(ch, col, j), s_y.at[k], y_sem.at[ch], (t, 1, r))
 
-        def own_a(ch):
-            @pl.when(kind(ch)[0])
+        def own_a(i, late):
+            ch, is_a, _, _, _ = kind(i, late)
+
+            @pl.when(is_a)
             def _():
                 across(ch, x, t, 0)
 
@@ -161,10 +162,10 @@
                 def _():
                     along(ch, t, False)
 
-        def own_z(ch):
-            is_a, _, is_g = kind(ch)
-
-            @pl.when(jnp.logical_not(is_a))
+        def own_z(i):
+            ch, _, _, is_g, not_a = kind(i, 0)
+
+            @pl.when(not_a)
             def _():
                 across(ch, x, t, 1)
 
@@ -172,58 +173,59 @@
             def _():
                 send(band(ch, x, t), band(ch, x, t), s_opp, x_sem.at[ch], (t, 0, r ^ 2))
 
-        def from_opp(ch):
-            @pl.when(kind(ch)[2])
+        def from_opp(i):
+            ch, _, _, is_g, _ = kind(i, 0)
+
+            @pl.when(is_g)
             def _():
                 wait(amount(1), x_sem.at[ch])
                 across(ch, 1 - x, t, 1)
 
-        def hop(k):
-            def body(ch):
-                is_a = kind(ch)[0]
-
-                @pl.when(jnp.logical_and(is_a, t >= k))
-                def _():
-                    wait(amount(1), b_sem.at[ch, t - k])
-                    across(ch, x, t - k, 0)
-
-                    @pl.when(t < 3)
-                    def _():
-                        along(ch, t - k, True)
-
-                @pl.when(jnp.logical_and(is_a, t + k <= 3))
-                def _():
-                    wait(amount(1), b_sem.at[ch, t + k])
-                    across(ch, x, t + k, 0)
-
-                    @pl.when(t > 0)
-                    def _():
-                        along(ch, t + k, False)
-
-            return body
+        def hop(i, late, k):
+            ch, is_a, _, _, _ = kind(i, late)
+
+            @pl.when(jnp.logical_and(is_a, t >= k))
+            def _():
+                wait(amount(1), b_sem.at[ch, t - k])
+                across(ch, x, t - k, 0)
+
+                @pl.when(t < 3)
+                def _():
+                    along(ch, t - k, True)
+
+            @pl.when(jnp.logical_and(is_a, t + k <= 3))
+            def _():
+                wait(amount(1), b_sem.at[ch, t + k])
+                across(ch, x, t + k, 0)
+
+                @pl.when(t > 0)
+                def _():
+                    along(ch, t + k, False)
 
         for cp in parts(0):
             cp.start()
 
-        def slot(b, done):
-            ya, yz = spans(b)[:2]
-            todo = (jnp.maximum(ya[1], yz[1]) + QS - 1) // QS
-            each((done, todo), update)
-            each(ya, own_a)
-            each(yz, own_z)
-
-            @pl.when(b == -B0)
-            def _():
-                for k in (1, 2, 3):
-                    each(ya, hop(k))
-
+        def slot(i, _):
+            @pl.when(jnp.logical_and(lax.rem(i, QS) == 0, i < NCH))
+            def _():
+                update(lax.div(i, QS))
+
+            @pl.when(jnp.logical_and(i == 0, jnp.logical_or(t == 1, t == 2)))
+            def _():
+                pl.semaphore_wait(barrier, 5)
+
+            @pl.when(jnp.logical_and(i == 0, jnp.logical_or(t == 0, t == 3)))
+            def _():
+                pl.semaphore_wait(barrier, 3)
+
+            own_a(i, T_AHEAD)
+            own_z(i)
             for k in (1, 2, 3):
-                lo, hi = spans(b - k)[0]
-                each((lo, jnp.where(b - k > -B0, hi, lo)), hop(k))
-            each(yz, from_opp)
-            return todo
-
-        lax.fori_loop(-B0, NCH + 4, slot, 0)
+                hop(i, T_AHEAD + k, k)
+            from_opp(i)
+            return 0
+
+        lax.fori_loop(0, NCH + T_AHEAD + 3, slot, 0)
 
         @pl.when(jnp.logical_or(t == 1, t == 2))
         def _():
@@ -256,6 +258,8 @@
     @pl.when(side == 1)
     def _():
         sib, opp = (t, 1, r ^ 1), (t, 1, r ^ 2)
+        greet_all(1)
+        greet(sib)
         base = jnp.where(t % 2 == 0, 0, R1)
 
         def over(ref, ch):
@@ -287,16 +291,18 @@
             send(own, own, s_opp, x_sem.at[ch], opp)
             over(own, ch)
 
-        def ya(ch):
-            @pl.when(kind(ch)[0])
+        def ya(i):
+            ch, is_a, _, _, _ = kind(i, YA)
+
+            @pl.when(is_a)
             def _():
                 wait(amount(4), y_sem.at[ch])
                 across(ch)
 
-        def yz(ch):
-            is_a, is_b, is_g = kind(ch)
-
-            @pl.when(jnp.logical_not(is_a))
+        def yz(i):
+            ch, _, is_b, is_g, not_a = kind(i, YZ)
+
+            @pl.when(not_a)
             def _():
                 arrive(y_sem.at[ch], is_b, is_g)
 
@@ -308,40 +314,39 @@
                 def _():
                     along(ch, t, False, is_b, is_g)
 
-        def hop(k):
-            def body(ch):
-                is_a, is_b, is_g = kind(ch)
-
-                @pl.when(jnp.logical_and(jnp.logical_not(is_a), t >= k))
-                def _():
-                    arrive(b_sem.at[ch, t - k], is_b, is_g)
-
-                    @pl.when(t < 3)
-                    def _():
-                        along(ch, t - k, True, is_b, is_g)
-
-                @pl.when(jnp.logical_and(jnp.logical_not(is_a), t + k <= 3))
-                def _():
-                    arrive(b_sem.at[ch, t + k], is_b, is_g)
-
-                    @pl.when(t > 0)
-                    def _():
-                        along(ch, t + k, False, is_b, is_g)
-
-                if k == 3:
-
-                    @pl.when(is_b)
-                    def _():
-                        across(ch)
-
-                    @pl.when(is_g)
-                    def _():
-                        over(w_all.at[ch, c], ch)
-
-            return body
-
-        def from_opp(ch):
-            @pl.when(jnp.logical_not(kind(ch)[2]))
+        def hop(i, k):
+            ch, _, is_b, is_g, not_a = kind(i, HOPS[k - 1])
+
+            @pl.when(jnp.logical_and(not_a, t >= k))
+            def _():
+                arrive(b_sem.at[ch, t - k], is_b, is_g)
+
+                @pl.when(t < 3)
+                def _():
+                    along(ch, t - k, True, is_b, is_g)
+
+            @pl.when(jnp.logical_and(not_a, t + k <= 3))
+            def _():
+                arrive(b_sem.at[ch, t + k], is_b, is_g)
+
+                @pl.when(t > 0)
+                def _():
+                    along(ch, t + k, False, is_b, is_g)
+
+            if k == 3:
+
+                @pl.when(is_b)
+                def _():
+                    across(ch)
+
+                @pl.when(is_g)
+                def _():
+                    over(w_all.at[ch, c], ch)
+
+        def from_opp(i):
+            ch, is_a, is_b, _, _ = kind(i, OPP)
+
+            @pl.when(jnp.logical_or(is_a, is_b))
             def _():
                 wait(amount(4), x_sem.at[ch])
                 over(w_all.at[ch, c, 1 - x], ch)
@@ -349,14 +354,21 @@
         def load(ch, ring):
             pltpu.make_async_copy(w_all.at[ch], wv.at[ring], ld_sem.at[ring]).start()
 
-        def ready(ch):
-            wait(amount(8), d_sem.at[ch])
-            load(ch, ch % (2 * QS))
-
-        def tick(b):
-            stages = (ya, yz, hop(1), hop(2), hop(3), from_opp, ready)
-            for span, stage in zip(spans(b), stages):
-                each(span, stage)
+        def ready(i):
+            @pl.when(jnp.logical_and(i >= DONE, i < NCH + DONE))
+            def _():
+                ch = jnp.clip(i - DONE, 0, NCH - 1)
+                wait(amount(8), d_sem.at[ch])
+                load(ch, lax.rem(ch, 2 * QS))
+
+        def tick(i):
+            ya(i)
+            hop(i, 3)
+            from_opp(i)
+            hop(i, 2)
+            yz(i)
+            hop(i, 1)
+            ready(i)
 
         def loaded(slot):
             for q in range(QS):
@@ -366,7 +378,7 @@
             return pltpu.make_async_copy(ref.at[pl.ds(row, n)], out.at[pl.ds(to, n)], o_sem)
 
         first = pltpu.make_async_copy(
-            rows_in.at[pl.ds(pl.multiple_of(base, 1024), R1)], h, h_sem.at[0]
+            rows_in.at[pl.ds(pl.multiple_of(base, 128), R1)], h, h_sem.at[0]
         )
         second = pltpu.make_async_copy(rows_in.at[pl.ds(2 * R1, R2)], h2, h_sem.at[1])
         first.start()
@@ -378,7 +390,8 @@
 
         lax.fori_loop(0, R1 // 128, zero, 0)
         first.wait()
-        lax.fori_loop(-B0, 0, lambda b, _: (tick(b), 0)[1], 0)
+        pl.semaphore_wait(barrier, 5)
+        lax.fori_loop(0, LEAD, lambda i, _: (tick(i), 0)[1], 0)
 
         def give(i):
             for q in range(M1 // PC):
@@ -443,7 +456,7 @@
 
             def block(i, _):
                 row = pl.multiple_of(i * M1, M1)
-                tick(QS * sp + i)
+                tick(LEAD + QS * sp + i)
 
                 @pl.when(sp < NST - 1)
                 def _():
@@ -496,7 +509,7 @@
                 @pl.when(sp == NST - 1)
                 def _():
                     multiply(h2, row, M2, slot, last=True)
-                    store(h2, row, M2, pl.multiple_of(2 * R1 + i * M2, M2)).start()
+                    store(h2, row, M2, pl.multiple_of(2 * R1 + i * M2, 128)).start()
 
                 return 0
 
@@ -678,7 +691,7 @@
             dma((2,)), dma((3,)), dma((NPC // 2,)),
         ],
         compiler_params=pltpu.CompilerParams(
-            has_side_effects=True, vmem_limit_bytes=67043328
+            has_side_effects=True, vmem_limit_bytes=67043328, collective_id=0
         ),
         name="sync_and_run",
     )(rate, wu, gu, wd, gd, rows)

time: 500 us -> 478 us (0.956)
  Pallas kernels: 498 us -> 476 us
    pallas_call x1, Pallas kernels: 472 us -> 450 us  [sync_and_run(): pl.pallas_call(kernel, out_shape=(jax.ShapeDtypeStruct((TOK, D), BF), jax...]
where the time goes in v3:
time: 478 us; the launch traced here: 477 us
  Pallas kernels  476 us (100%)
    pallas_call x1, Pallas kernels, sync_and_run(): pl.pallas_call(kernel, out_shape=(jax.ShapeDtypeStruct((TOK, D), BF), jax...  450 us
    pallas_call x1, Pallas kernels, finalize(): pl.pallas_call(finalize_kernel, out_shape=(jax.ShapeDtypeStruct((128, F),...  26 us

profile of v3, /device:TPU:4, one launch (start us, length us, event | category | flops | bytes accessed | tf_op | source)
XLA Modules:
  0.0 477.1 jit_solution(9294429949132776412)
XLA Ops:
  1.3 449.6 %sync_and_run.1 = (bf16[8192,2048]{1,0:T(8,128)(2,1)}, bf16[64,2,2,2,512,128]{5,4,3,2,1,0:T(8,128)(2,1)}, bf16[20,80,2048]{2,1,0:T(8,128)(2,1)}) custom-call(f32[1]{0:T(128)S(6)} %copy.9.rate, f32[128,8192]{1,0:T(8,128)} %bitcast.9, f32[128,8192]{1,0:T(8,128)} %bitcast.11, f32[8192,128]{1,0:T(8,128)} %bitcast.13, f32[8192,128]{1,0:T(8,128)} %bitcast.15, ...), custom_call_target="tpu_custom_call" | custom-call | tf_op jit(solution)/shard_map/sync_and_run/pallas_call | solution.py:674
  450.9 26.0 %finalize.1 = (f32[128,8192]{1,0:T(8,128)}, f32[8192,128]{1,0:T(8,128)}, bf16[8192,2048]{1,0:T(8,128)(2,1)}) custom-call(f32[1]{0:T(128)S(6)} %copy.9.rate, f32[128,8192]{1,0:T(8,128)} %bitcast.10, f32[128,8192]{1,0:T(8,128)} %bitcast.12, f32[8192,128]{1,0:T(8,128)} %bitcast.14, f32[8192,128]{1,0:T(8,128)} %bitcast.16, bf16[8192,2048]{1,0:T(8,128)(2,1)} %get-tuple-element.7.res), custom_call_target="tpu_custom_call" | custom-call | tf_op jit(solution)/shard_map/finalize/pallas_call | solution.py:649

commit v4 on v3

--- a/solution.py
+++ b/solution.py
@@ -19,8 +19,9 @@
 R1 = QS * M1
 R2 = TOK - 2 * R1
 M2 = R2 // 2
-PC = 80
+PC = 40
 NPC = R1 // PC
+VIA = NPC // 2 - 1
 N_A, N_B, MUL, OFF = 29, 12, 23, 17
 N_G = NCH - N_A - N_B
 LEAD = 13
@@ -239,7 +240,7 @@
                 send(relay.at[i], out.at[pl.ds(row, PC)], e_send.at[2], e_recv.at[odd], (end, 1, r))
                 return 0
 
-            lax.fori_loop(0, NPC // 2, piece, 0)
+            lax.fori_loop(0, VIA, piece, 0)
             wait(relay, e_send.at[2])
 
         wait(amount(4 * N_A), s_y.at[0])
@@ -374,9 +375,6 @@
             for q in range(QS):
                 wait(wv.at[QS * slot + q], ld_sem.at[QS * slot + q])
 
-        def store(ref, row, n, to):
-            return pltpu.make_async_copy(ref.at[pl.ds(row, n)], out.at[pl.ds(to, n)], o_sem)
-
         first = pltpu.make_async_copy(
             rows_in.at[pl.ds(pl.multiple_of(base, 128), R1)], h, h_sem.at[0]
         )
@@ -394,31 +392,31 @@
         lax.fori_loop(0, LEAD, lambda i, _: (tick(i), 0)[1], 0)
 
         def give(i):
-            for q in range(M1 // PC):
-                p = i * (M1 // PC) + q
-                src = out.at[pl.ds(pl.multiple_of(base + p * PC, PC), PC)]
-                i2 = i * (M1 // PC // 2) + q // 2
-                if q % 2 == 0:
-
-                    @pl.when(t < 3)
+            def pieces(q, _):
+                i2 = i * (M1 // PC // 2) + q
+                right, left = (t + 1, 1, r), (t - 1, 1, r)
+                for odd in range(2):
+                    row = pl.multiple_of(base + (2 * i2 + odd) * PC, PC)
+                    src = out.at[pl.ds(row, PC)]
+
+                    @pl.when(t > 0 if odd else t < 3)
                     def _():
-                        send(src, src, e_send.at[0], e_recv.at[0], (t + 1, 1, r))
-
-                    @pl.when(t == 1)
+                        send(src, src, e_send.at[odd], e_recv.at[odd], left if odd else right)
+
+                    @pl.when(jnp.logical_and(t == 1 + odd, i2 < VIA))
                     def _():
-                        send(src, relay.at[i2], e_send.at[2], r_recv.at[i2], (t, 0, r))
-                else:
-
-                    @pl.when(t > 0)
+                        to = jnp.minimum(i2, VIA - 1)
+                        send(src, relay.at[to], e_send.at[2], r_recv.at[to], (t, 0, r))
+
+                    @pl.when(jnp.logical_and(t == 1 + odd, i2 >= VIA))
                     def _():
-                        send(src, src, e_send.at[1], e_recv.at[1], (t - 1, 1, r))
-
-                    @pl.when(t == 2)
-                    def _():
-                        send(src, relay.at[i2], e_send.at[2], r_recv.at[i2], (t, 0, r))
-
-        def multiply(ref, row, m, slot, first=False, last=False):
-            rs = pl.ds(row, m)
+                        send(src, src, e_send.at[3], e_recv.at[odd], right if odd else left)
+
+                return 0
+
+            lax.fori_loop(0, M1 // PC // 2, pieces, 0)
+
+        def multiply(ref, rows, slot, first=False, last=None):
             up = jnp.concatenate(
                 [
                     jnp.concatenate([wv[QS * slot + q, k % 2, k // 2, 0] for q in range(QS)], axis=1)
@@ -426,9 +424,9 @@
                 ],
                 axis=0,
             )
-            u = gelu(jnp.dot(ref[rs, :], up, preferred_element_type=F32)).astype(BF)
-            for k in range(4):
-                down = jnp.concatenate(
+
+            def down(k):
+                return jnp.concatenate(
                     [
                         jnp.concatenate(
                             [
@@ -441,82 +439,74 @@
                     ],
                     axis=1,
                 )
-                cs = pl.ds(k * 512, 512)
-                part = jnp.dot(u, down, preferred_element_type=F32)
-                if last:
-                    ref[rs, cs] = (ref[rs, cs].astype(F32) + (acc[rs, cs] + part)).astype(BF)
-                elif first:
-                    acc[rs, cs] = part
-                else:
-                    acc[rs, cs] += part
+
+            pre = jnp.dot(ref[rows[0], :], up, preferred_element_type=F32)
+            for n, rs in enumerate(rows):
+                if n + 1 < len(rows):
+                    ahead = jnp.dot(ref[rows[n + 1], :], up, preferred_element_type=F32)
+                u = gelu(pre).astype(BF)
+                for k in range(4):
+                    cs = pl.ds(k * 512, 512)
+                    part = jnp.dot(u, down(k), preferred_element_type=F32)
+                    if last is not None:
+                        ref[rs, cs] = (ref[rs, cs].astype(F32) + (acc[rs, cs] + part)).astype(BF)
+                        to = out.at[pl.ds(last[n], rs.size), cs]
+                        pltpu.make_async_copy(ref.at[rs, cs], to, o_sem).start()
+                    elif first:
+                        acc[rs, cs] = part
+                    else:
+                        acc[rs, cs] += part
+                pre = ahead if n + 1 < len(rows) else None
 
         def step1(sp, _):
             slot = lax.rem(sp, 2)
             loaded(slot)
 
             def block(i, _):
-                row = pl.multiple_of(i * M1, M1)
                 tick(LEAD + QS * sp + i)
-
-                @pl.when(sp < NST - 1)
-                def _():
-                    multiply(h, row, M1, slot)
-
-                @pl.when(sp == NST - 1)
-                def _():
-                    load(i, i)
-
-                    @pl.when(i > 0)
-                    def _():
-                        wait(h.at[pl.ds(0, M1)], o_sem)
-                        give(i - 1)
-
-                    multiply(h, row, M1, slot, last=True)
-                    store(h, row, M1, pl.multiple_of(base + i * M1, M1)).start()
-
+                multiply(h, [pl.ds(pl.multiple_of(i * M1, M1), M1)], slot)
                 return 0
 
             lax.fori_loop(0, R1 // M1, block, 0)
             return 0
 
-        lax.fori_loop(0, NST, step1, 0)
+        lax.fori_loop(0, NST - 1, step1, 0)
+        loaded(1)
+
+        def last1(i, _):
+            load(i, i)
+
+            @pl.when(i > 0)
+            def _():
+                wait(h.at[pl.ds(0, M1)], o_sem)
+                give(i - 1)
+
+            row = pl.multiple_of(i * M1, M1)
+            multiply(h, [pl.ds(row, M1)], 1, last=[pl.multiple_of(base + i * M1, M1)])
+            return 0
+
+        lax.fori_loop(0, R1 // M1, last1, 0)
         second.wait()
         loaded(0)
         for q in range(QS):
             load(QS + q, QS + q)
-        for i in range(R2 // M2):
-            multiply(h2, i * M2, M2, 0, first=True)
-            if i == 0:
-                wait(h.at[pl.ds(0, M1)], o_sem)
-                give(R1 // M1 - 1)
+        wait(h.at[pl.ds(0, M1)], o_sem)
+        give(R1 // M1 - 1)
+        halves = [pl.ds(0, M2), pl.ds(M2, M2)]
+        multiply(h2, halves, 0, first=True)
 
         def step2(sp, _):
             slot = lax.rem(sp, 2)
             loaded(slot)
-
-            @pl.when(sp < NST - 1)
-            def _():
-                for q in range(QS):
-                    load(QS * (sp + 1) + q, QS * (1 - slot) + q)
-
-            def block(i, _):
-                row = pl.multiple_of(i * M2, M2)
-
-                @pl.when(sp < NST - 1)
-                def _():
-                    multiply(h2, row, M2, slot)
-
-                @pl.when(sp == NST - 1)
-                def _():
-                    multiply(h2, row, M2, slot, last=True)
-                    store(h2, row, M2, pl.multiple_of(2 * R1 + i * M2, 128)).start()
-
-                return 0
-
-            lax.fori_loop(0, R2 // M2, block, 0)
+            for q in range(QS):
+                load(QS * (sp + 1) + q, QS * (1 - slot) + q)
+
+            multiply(h2, halves, slot)
             return 0
 
-        lax.fori_loop(1, NST, step2, 0)
+        lax.fori_loop(1, NST - 1, step2, 0)
+        loaded(1)
+        multiply(h2, halves, 1, last=[2 * R1, 2 * R1 + M2])
         wait(h2, o_sem)
 
         half_rows = out.at[pl.ds(0, R1 // 2)]
@@ -533,7 +523,8 @@
 
         @pl.when(jnp.logical_or(t == 1, t == 2))
         def _():
-            wait(half_rows, e_send.at[2])
+            wait(out.at[pl.ds(0, VIA * PC)], e_send.at[2])
+            wait(out.at[pl.ds(0, R1 // 2 - VIA * PC)], e_send.at[3])
 
         wait(amount(8 * NCH), s_over)
         wait(amount(4 * (N_A + N_B)), s_opp)
@@ -676,7 +667,7 @@
         out_shape=(
             jax.ShapeDtypeStruct((TOK, D), BF),
             jax.ShapeDtypeStruct((NCH, 2, 2, 2, 512, FC), BF),
-            jax.ShapeDtypeStruct((NPC // 2, PC, D), BF),
+            jax.ShapeDtypeStruct((VIA, PC, D), BF),
         ),
         in_specs=[pl.BlockSpec(memory_space=pltpu.SMEM)] + [any_] * 5,
         out_specs=(any_,) * 3,
@@ -688,7 +679,7 @@
             dma((NCH,)), dma((NCH,)), dma((NCH, 4)), dma((NCH,)),
             dma(()), dma(()), dma((2,)), dma((2, 2)),
             dma((2 * QS,)), dma((2, 4)), dma((2,)), dma(()),
-            dma((2,)), dma((3,)), dma((NPC // 2,)),
+            dma((2,)), dma((4,)), dma((VIA,)),
         ],
         compiler_params=pltpu.CompilerParams(
             has_side_effects=True, vmem_limit_bytes=67043328, collective_id=0

time: 478 us -> 469 us (0.981)
  Pallas kernels: 476 us -> 467 us
    pallas_call x1, Pallas kernels: 450 us -> 441 us  [sync_and_run(): pl.pallas_call(kernel, out_shape=(jax.ShapeDtypeStruct((TOK, D), BF), jax...]
where the time goes in v4:
time: 469 us; the launch traced here: 468 us
  Pallas kernels  467 us (100%)
    pallas_call x1, Pallas kernels, sync_and_run(): pl.pallas_call(kernel, out_shape=(jax.ShapeDtypeStruct((TOK, D), BF), jax...  441 us
    pallas_call x1, Pallas kernels, finalize(): pl.pallas_call(finalize_kernel, out_shape=(jax.ShapeDtypeStruct((128, F),...  26 us

profile of v4, /device:TPU:4, one launch (start us, length us, event | category | flops | bytes accessed | tf_op | source)
XLA Modules:
  0.0 468.1 jit_solution(17958726201292372409)
XLA Ops:
  1.3 440.5 %sync_and_run.1 = (bf16[8192,2048]{1,0:T(8,128)(2,1)}, bf16[64,2,2,2,512,128]{5,4,3,2,1,0:T(8,128)(2,1)}, bf16[39,40,2048]{2,1,0:T(8,128)(2,1)}) custom-call(f32[1]{0:T(128)S(6)} %copy.9.rate, f32[128,8192]{1,0:T(8,128)} %bitcast.9, f32[128,8192]{1,0:T(8,128)} %bitcast.11, f32[8192,128]{1,0:T(8,128)} %bitcast.13, f32[8192,128]{1,0:T(8,128)} %bitcast.15, ...), custom_call_target="tpu_custom_call" | custom-call | tf_op jit(solution)/shard_map/sync_and_run/pallas_call | solution.py:665
  441.8 26.0 %finalize.1 = (f32[128,8192]{1,0:T(8,128)}, f32[8192,128]{1,0:T(8,128)}, bf16[8192,2048]{1,0:T(8,128)(2,1)}) custom-call(f32[1]{0:T(128)S(6)} %copy.9.rate, f32[128,8192]{1,0:T(8,128)} %bitcast.10, f32[128,8192]{1,0:T(8,128)} %bitcast.12, f32[8192,128]{1,0:T(8,128)} %bitcast.14, f32[8192,128]{1,0:T(8,128)} %bitcast.16, bf16[8192,2048]{1,0:T(8,128)(2,1)} %get-tuple-element.7.res), custom_call_target="tpu_custom_call" | custom-call | tf_op jit(solution)/shard_map/finalize/pallas_call | solution.py:640

commit v5 on v4

--- a/solution.py
+++ b/solution.py
@@ -21,6 +21,7 @@
 M2 = R2 // 2
 PC = 40
 NPC = R1 // PC
+BPC = M1 // PC // 2
 VIA = NPC // 2 - 1
 N_A, N_B, MUL, OFF = 29, 12, 23, 17
 N_G = NCH - N_A - N_B
@@ -236,7 +237,8 @@
 
             def piece(i, _):
                 wait(relay.at[i], r_recv.at[i])
-                row = pl.multiple_of(base + (2 * i + odd) * PC, PC)
+                half = lax.div(i, BPC) * M1 + odd * (M1 // 2)
+                row = pl.multiple_of(base + half + lax.rem(i, BPC) * PC, PC)
                 send(relay.at[i], out.at[pl.ds(row, PC)], e_send.at[2], e_recv.at[odd], (end, 1, r))
                 return 0
 
@@ -392,29 +394,33 @@
         lax.fori_loop(0, LEAD, lambda i, _: (tick(i), 0)[1], 0)
 
         def give(i):
-            def pieces(q, _):
-                i2 = i * (M1 // PC // 2) + q
-                right, left = (t + 1, 1, r), (t - 1, 1, r)
-                for odd in range(2):
-                    row = pl.multiple_of(base + (2 * i2 + odd) * PC, PC)
-                    src = out.at[pl.ds(row, PC)]
-
-                    @pl.when(t > 0 if odd else t < 3)
-                    def _():
-                        send(src, src, e_send.at[odd], e_recv.at[odd], left if odd else right)
-
-                    @pl.when(jnp.logical_and(t == 1 + odd, i2 < VIA))
-                    def _():
-                        to = jnp.minimum(i2, VIA - 1)
-                        send(src, relay.at[to], e_send.at[2], r_recv.at[to], (t, 0, r))
-
-                    @pl.when(jnp.logical_and(t == 1 + odd, i2 >= VIA))
-                    def _():
-                        send(src, src, e_send.at[3], e_recv.at[odd], right if odd else left)
-
-                return 0
-
-            lax.fori_loop(0, M1 // PC // 2, pieces, 0)
+            for odd, (dev, there) in enumerate((((t + 1, 1, r), t < 3), ((t - 1, 1, r), t > 0))):
+                row = pl.multiple_of(base + i * M1 + odd * (M1 // 2), M1 // 2)
+                src = out.at[pl.ds(row, M1 // 2)]
+
+                @pl.when(there)
+                def _():
+                    send(src, src, e_send.at[odd], e_recv.at[odd], dev)
+
+                @pl.when(t == 1 + odd)
+                def _():
+                    def piece(q, _):
+                        i2 = i * BPC + q
+                        part = out.at[pl.ds(pl.multiple_of(row + q * PC, PC), PC)]
+
+                        @pl.when(i2 < VIA)
+                        def _():
+                            to = jnp.minimum(i2, VIA - 1)
+                            send(part, relay.at[to], e_send.at[2], r_recv.at[to], (t, 0, r))
+
+                        @pl.when(i2 >= VIA)
+                        def _():
+                            end = (t + 1, 1, r) if odd else (t - 1, 1, r)
+                            send(part, part, e_send.at[3], e_recv.at[odd], end)
+
+                        return 0
+
+                    lax.fori_loop(0, BPC, piece, 0)
 
         def multiply(ref, rows, slot, first=False, last=None):
             up = jnp.concatenate(
@@ -490,10 +496,10 @@
         loaded(0)
         for q in range(QS):
             load(QS + q, QS + q)
+        halves = [pl.ds(0, M2), pl.ds(M2, M2)]
+        multiply(h2, halves, 0, first=True)
         wait(h.at[pl.ds(0, M1)], o_sem)
         give(R1 // M1 - 1)
-        halves = [pl.ds(0, M2), pl.ds(M2, M2)]
-        multiply(h2, halves, 0, first=True)
 
         def step2(sp, _):
             slot = lax.rem(sp, 2)
@@ -540,7 +546,7 @@
                     wait(amount((4 - tt) * 2 * N_G), s_z.at[1, 1])
 
 
-CR, RING = 512, 8
+CR = 1024
 
 
 def finalize_kernel(
@@ -554,26 +560,22 @@
     @pl.when(side == 1)
     def _():
         def read(i):
-            return copy(res.at[pl.ds(i * CR, CR)], buf.at[i % RING], r_sem.at[i % RING])
+            return copy(res.at[pl.ds(i * CR, CR)], buf.at[i], r_sem.at[i])
 
         def write(i):
-            return copy(buf.at[i % RING], out.at[pl.ds(i * CR, CR)], w_sem.at[i % RING])
-
-        n = TOK // CR
-        for i in range(RING // 2):
+            return copy(buf.at[i], out.at[pl.ds(i * CR, CR)], w_sem.at[i])
+
+        for i in range(TOK // CR):
             read(i).start()
         zero[...] = jnp.zeros_like(zero)
+        for i in range(TOK // CR):
+            read(i).wait()
+        for i in range(TOK // CR):
+            write(i).start()
         for i in range(8):
             copy(zero.at[pl.ds(0, 128)], up_out.at[:, pl.ds(i * 1024, 1024)], u_sem.at[0, 0]).start()
             copy(zero.at[:, pl.ds(0, 128)], dn_out.at[pl.ds(i * 1024, 1024)], u_sem.at[0, 1]).start()
-        for i in range(n):
-            if i + RING // 2 < n:
-                if i >= RING // 2:
-                    write(i - RING // 2).wait()
-                read(i + RING // 2).start()
-            read(i).wait()
-            write(i).start()
-        for i in range(n - RING, n):
+        for i in range(TOK // CR):
             write(i).wait()
         copy(up_out, up_out, u_sem.at[0, 0]).wait()
         copy(dn_out, dn_out, u_sem.at[0, 1]).wait()
@@ -647,12 +649,12 @@
         in_specs=[pl.BlockSpec(memory_space=pltpu.SMEM)] + [any_] * 5,
         out_specs=(any_,) * 3,
         scratch_shapes=[
-            pltpu.VMEM((RING, CR, D), BF),
+            pltpu.VMEM((TOK // CR, CR, D), BF),
             pltpu.VMEM((1024, 1024), F32),
             pltpu.VMEM((CR, D), BF),
             pltpu.VMEM((2, 3, 128, QS * FC), F32),
             pltpu.VMEM((2, 3, QS * FC, 128), F32),
-            dma((RING,)), dma((RING,)), dma((2, 4)), dma((2, 2)),
+            dma((TOK // CR,)), dma((TOK // CR,)), dma((2, 4)), dma((2, 2)),
         ],
         compiler_params=pltpu.CompilerParams(vmem_limit_bytes=60 << 20),
         name="finalize",

time: 469 us -> 466 us (level)
  no operation moved by 1% of the time
where the time goes in v5:
time: 466 us; the launch traced here: 465 us
  Pallas kernels  464 us (100%)
    pallas_call x1, Pallas kernels, sync_and_run(): pl.pallas_call(kernel, out_shape=(jax.ShapeDtypeStruct((TOK, D), BF), jax...  439 us
    pallas_call x1, Pallas kernels, finalize(): pl.pallas_call(finalize_kernel, out_shape=(jax.ShapeDtypeStruct((128, F),...  24.3 us

profile of v5, /device:TPU:4, one launch (start us, length us, event | category | flops | bytes accessed | tf_op | source)
XLA Modules:
  0.0 465.1 jit_solution(5554583431628451962)
XLA Ops:
  1.3 439.4 %sync_and_run.1 = (bf16[8192,2048]{1,0:T(8,128)(2,1)}, bf16[64,2,2,2,512,128]{5,4,3,2,1,0:T(8,128)(2,1)}, bf16[39,40,2048]{2,1,0:T(8,128)(2,1)}) custom-call(f32[1]{0:T(128)S(6)} %copy.9.rate, f32[128,8192]{1,0:T(8,128)} %bitcast.9, f32[128,8192]{1,0:T(8,128)} %bitcast.11, f32[8192,128]{1,0:T(8,128)} %bitcast.13, f32[8192,128]{1,0:T(8,128)} %bitcast.15, ...), custom_call_target="tpu_custom_call" | custom-call | tf_op jit(solution)/shard_map/sync_and_run/pallas_call | solution.py:667
  440.7 24.3 %finalize.1 = (f32[128,8192]{1,0:T(8,128)}, f32[8192,128]{1,0:T(8,128)}, bf16[8192,2048]{1,0:T(8,128)(2,1)}) custom-call(f32[1]{0:T(128)S(6)} %copy.9.rate, f32[128,8192]{1,0:T(8,128)} %bitcast.10, f32[128,8192]{1,0:T(8,128)} %bitcast.12, f32[8192,128]{1,0:T(8,128)} %bitcast.14, f32[8192,128]{1,0:T(8,128)} %bitcast.16, bf16[8192,2048]{1,0:T(8,128)(2,1)} %get-tuple-element.7.res), custom_call_target="tpu_custom_call" | custom-call | tf_op jit(solution)/shard_map/finalize/pallas_call | solution.py:642
